TPU v7x, 256 devices: a whole 4x4x8 slice. The times are simulated.
256 devices in a mesh: row: 16 (over x, z_hi, core), col: 16 (over z_lo, y).
Axes of the slice: x: 4, y: 4, z: 8 (z_hi: 2, z_lo: 4; z = z_hi * 4 + z_lo), core: 2. Of those that a mesh axis runs over, the one named last changes fastest.
Arguments:
- state: float32 [512, 65536], P(None, ('row', 'col')), may hold values from -6 to 6
- obs_index: int32 [2, 512], replicated, may hold values from 0 to 65535
- obs_values: float32 [2, 512], replicated, may hold values from -6 to 6
- obs_var: float32 [2, 512], replicated, may hold values from 0.3 to 3
- noise: float32 [2, 512, 512], P(None, None, 'col'), may hold values from -6 to 6
Outputs:
- analysis: float32 [512, 65536], P(None, ('row', 'col'))
All inputs are finite; a program needn't handle non-finite values.
Results may differ from a plain program's by a relative error of at most 0.0001.
Values sent between devices are 32-bit elements; how exact they have to be, the bound alone decides.
No kernel may reach another device: no remote copies, remote signals or barrier semaphores. Data moves between devices by JAX's collectives and lax.ppermute only.
A program may use at most 64 MiB of HBM per device.

v0:
```python
import functools

import jax
import jax.numpy as jnp
from jax import lax
from jax.experimental import pallas as pl
from jax.experimental.pallas import tpu as pltpu
from jax.sharding import Mesh
from jax.sharding import PartitionSpec as P


POSITIONS = 256
RADIUS = 64
ROW = ("x", "zh", "core")
COL = ("zl", "y")
ROW_COL = ROW + COL
SLOTS = 4

f32 = jnp.float32
bf16 = jnp.bfloat16
i32 = jnp.int32


def nn(a, b):
    return lax.dot_general(a, b, (((1,), (0,)), ((), ())), preferred_element_type=f32)


def nt(a, b):
    return lax.dot_general(a, b, (((1,), (1,)), ((), ())), preferred_element_type=f32)


def split2(x):
    high = x.astype(bf16)
    return high, (x - high.astype(f32)).astype(bf16)


def split3(x):
    high = x.astype(bf16)
    rest = x - high.astype(f32)
    middle = rest.astype(bf16)
    return high, middle, (rest - middle.astype(f32)).astype(bf16)


def one_hot(mask):
    return jnp.where(mask, 1.0, 0.0).astype(bf16)


def exact_nn(hot, x):
    high, middle, low = split3(x)
    return nn(hot, high) + nn(hot, middle) + nn(hot, low)


def exact_nt(hot, x):
    high, middle, low = split3(x)
    return nt(hot, high) + nt(hot, middle) + nt(hot, low)


def exact_tn(x, hot):
    high, middle, low = split3(x)
    return nt(high, hot) + nt(middle, hot) + nt(low, hot)


def column_of(row):
    return jnp.broadcast_to(row, (128, row.shape[1])).T[:, 0:1]


def iota(shape, dim):
    return lax.broadcasted_iota(i32, shape, dim)


def shift_of(value):
    assert value & (value - 1) == 0
    return value.bit_length() - 1


def right(value, bits):
    return lax.shift_right_logical(value, jnp.full(value.shape, bits, i32))


def order_of(rows, tile_rows, obs):
    tile = right(rows, shift_of(tile_rows))
    key = (tile * obs + iota((1, obs), 1)).astype(f32)
    rank = jnp.sum(jnp.where(column_of(key) < key, 1.0, 0.0), axis=0, keepdims=True)
    rank = rank.astype(i32)
    return tile, rank


def par_kernel(dims, where_ref, index_ref, values_ref, var_ref, noise_ref, par_ref, noise_out_ref):
    bin_rows, tile_rows, cols = dims
    batches, obs = index_ref.shape
    for b in range(batches):
        rows = index_ref[b:b + 1, :]
        _, rank = order_of(rows, tile_rows, obs)
        placed = (rank & (cols - 1)) * (obs // cols) + right(rank, shift_of(cols))
        hot = one_hot(iota((obs, obs), 0) == placed)
        par = jnp.concatenate(
            [right(rows, shift_of(bin_rows)).astype(f32), values_ref[b:b + 1, :],
             var_ref[b:b + 1, :], jnp.zeros((5, obs), f32)], axis=0)
        par_ref[4 * b:4 * b + 4, :] = exact_tn(par, hot)[0:4]
        noise_out_ref[b] = exact_tn(noise_ref[b], hot)


def send_kernel(dims, where_ref, index_ref, state_ref, send_ref):
    tile_rows, _, cols = dims
    _, rows_dev = state_ref.shape
    batches, obs = index_ref.shape
    my_tile, first, turn = where_ref[0], where_ref[1], where_ref[2]
    slots = send_ref.shape[0]
    per_col = slots // cols
    pick = jnp.zeros((slots, rows_dev), f32)
    for b in range(batches):
        rows = index_ref[b:b + 1, :]
        tile, rank = order_of(rows, tile_rows, obs)
        col = rank & (cols - 1)
        start = jnp.sum(jnp.where(tile < my_tile, 1.0, 0.0), axis=1, keepdims=True).astype(i32)
        base = start + ((col - start) & (cols - 1))
        turn_slot = right(rank - base + 16 * cols * obs, shift_of(cols)) - 16 * obs - turn * SLOTS
        local = rows - first
        inside = (local >= 0) & (local < rows_dev) & (turn_slot >= 0) & (turn_slot < SLOTS)
        slot = jnp.where(inside, col * per_col + b * SLOTS + turn_slot, -1)
        pick += nt(one_hot(iota((slots, obs), 0) == slot),
                   one_hot(iota((rows_dev, obs), 0) == local))
    send_ref[...] = exact_nt(pick.astype(bf16), state_ref[...])


def place_kernel(dims, where_ref, index_ref, slots_ref, held_ref, out_ref):
    tile_rows, cols, sizes = dims
    batches, _ = index_ref.shape
    slots = slots_ref.shape[0]
    my_col, turn = where_ref[0], where_ref[1]
    mine = [where_ref[2 + k] for k in range(3)]
    half = out_ref.shape[0] // batches
    p = iota((slots, 1), 0)
    block = right(p, shift_of(batches * SLOTS))
    batch = right(p, shift_of(SLOTS)) & (batches - 1)
    slot = (p & (SLOTS - 1)) + turn * SLOTS
    nx, nz, nc = sizes
    block_z = block & (nz - 1)
    block_x = right(block, shift_of(nz)) & (nx - 1)
    block_c = right(block, shift_of(nz * nx))
    tile_p = (((mine[0] - block_x) & (nx - 1)) * nz + ((mine[1] - block_z) & (nz - 1))) * nc
    tile_p = tile_p + ((mine[2] - block_c) & (nc - 1))
    start = jnp.zeros((slots, 1), i32)
    end = jnp.zeros((slots, 1), i32)
    for b in range(batches):
        tile = right(index_ref[b:b + 1, :], shift_of(tile_rows))
        before = jnp.sum(jnp.where(tile < tile_p, 1.0, 0.0), axis=1, keepdims=True).astype(i32)
        through = jnp.sum(jnp.where(tile <= tile_p, 1.0, 0.0), axis=1, keepdims=True).astype(i32)
        start = jnp.where(batch == b, before, start)
        end = jnp.where(batch == b, through, end)
    rank = start + ((my_col - start) & (cols - 1)) + slot * cols
    j = right(rank - my_col, shift_of(cols)) - mine[2] * half
    target = jnp.where((rank < end) & (j >= 0) & (j < half), batch * half + j, -1)
    wide = 128
    hot = jnp.where(iota((slots, wide), 1) == target, 1.0, 0.0).T.astype(bf16)
    out_ref[...] = held_ref[...] + exact_nn(hot[0:out_ref.shape[0]], slots_ref[...])


def taper(first, second):
    scaled = (first - second) * (1.0 / RADIUS)
    return jnp.exp(-0.5 * scaled * scaled)


def put_in_place(where, source_a, source_b, target, skip, stride, nzl, ny):
    zl, y, core = where
    unit = target.shape[0] // (2 * nzl * ny)
    for source, half in ((source_a, core), (source_b, 1 - core)):
        for dy in range(ny):
            for dz in range(nzl):
                at = ((((zl - dz) & (nzl - 1)) * ny + ((y - dy) & (ny - 1))) * 2 + half) * unit
                k = ((dy * nzl + dz) * stride + skip) * unit
                target[pl.ds(pl.multiple_of(at, unit), unit), :] = source[k:k + unit, :]


def pieces(size, width, body, carry=0):
    def step(k, carry):
        at = k * width
        return body(pl.ds(pl.multiple_of(at, width), width), at, carry)

    return lax.fori_loop(0, size // width, step, carry)


def each(size, width, body):
    def step(ds, at, carry):
        body(ds, at)
        return carry

    pieces(size, width, step)


def eye_part(obs, width, at):
    return iota((obs, width), 0) == iota((obs, width), 1) + at


def ident_part(obs, width, at):
    return jnp.where(eye_part(obs, width, at), 1.0, 0.0)


def centre(o, high, middle, low):
    def rows(ds, at):
        part = o[ds, :]
        part = part - jnp.mean(part, axis=1, keepdims=True)
        high[ds, :], middle[ds, :], low[ds, :] = split3(part)

    each(o.shape[0], 128, rows)


def invert(pos_r, var_r, pos_c, members, high, middle, low, left, gram, other, spare, s_high, s_low,
           xa, xb, ra, rb, eh, el, vec):
    obs = gram.shape[0]
    width = obs // 2
    norming = 1.0 / (members - 1)

    def cross_terms(ds, at):
        left[:, ds] = nt(high[...], middle[ds, :]) + nt(high[...], low[ds, :])

    each(obs, width, cross_terms)

    def covariance(ds, at):
        product = nt(high[...], high[ds, :]) + nt(middle[...], middle[ds, :])
        product = product + left[:, ds] + left[ds, :].T
        eye = eye_part(obs, width, at)
        covar = taper(pos_c, pos_r[:, ds]) * product * norming + jnp.where(eye, var_r[:, ds], 0.0)
        gram[:, ds] = covar
        vec[0:1, ds] = lax.rsqrt(jnp.sum(jnp.where(eye, covar, 0.0), axis=0, keepdims=True))

    each(obs, width, covariance)
    scale_c = column_of(vec[0:1, :])

    def rescale(ds, at):
        scaled = gram[:, ds] * scale_c * vec[0:1, ds]
        gram[:, ds] = scaled
        s_high[:, ds], s_low[:, ds] = split2(scaled)

    each(obs, width, rescale)

    def squared(ds, at):
        square = nn(s_high[...], s_high[:, ds])
        left[:, ds] = square
        vec[1:2, ds] = jnp.sum(jnp.abs(square), axis=0, keepdims=True)

    each(obs, width, squared)
    upper = jnp.sqrt(jnp.max(vec[1:2, :], axis=1, keepdims=True)) * 1.01
    lower = jnp.min(var_r[...] * vec[0:1, :] * vec[0:1, :], axis=1, keepdims=True)
    alpha = 2.0 / (upper + lower)

    def widen(low_end):
        image = low_end * (2.0 - low_end)
        factor = 2.0 / (1.0 + image)
        return factor, factor * image

    factor, low_end = widen(alpha * lower)

    def first(ds, at):
        ident = ident_part(obs, width, at)
        step = alpha * gram[:, ds]
        xa[:, ds] = (factor * alpha * (2.0 * ident - step)).astype(bf16)
        ra[:, ds] = (ident - factor * (2.0 * step - alpha * alpha * left[:, ds])).astype(bf16)

    each(obs, width, first)

    def grow(old, new, factor):
        def part(ds, at):
            new[:, ds] = (factor * (old[:, ds].astype(f32) + nn(old[...], ra[:, ds]))).astype(bf16)

        each(obs, width, part)

    def remain(new):
        def part(ds, at):
            ra[:, ds] = (ident_part(obs, width, at) - nn(s_high[...], new[:, ds])).astype(bf16)

        each(obs, width, part)

    factor, low_end = widen(low_end)
    grow(xa, xb, factor)
    remain(xb)
    factor, low_end = widen(low_end)
    grow(xb, xa, factor)
    remain(xa)
    factor, low_end = widen(low_end)
    grow(xa, xb, factor)

    def remain_last(ds, at):
        residual = (ident_part(obs, width, at)
                    - nn(s_high[...], xb[:, ds]) - nn(s_low[...], xb[:, ds]))
        left[:, ds] = residual
        ra[:, ds] = residual.astype(bf16)
        vec[1:2, ds] = jnp.sum(jnp.abs(residual), axis=0, keepdims=True)

    each(obs, width, remain_last)

    def second_order(ds, at):
        rb[:, ds] = (left[:, ds] + nn(ra[...], ra[:, ds])).astype(bf16)

    each(obs, width, second_order)

    def correction(ds, at):
        eh[:, ds], el[:, ds] = split2(nn(xb[...], rb[:, ds]))

    each(obs, width, correction)
    size = jnp.max(vec[1:2, :], axis=1, keepdims=True)

    @pl.when(jnp.logical_not(size[0, 0] < 0.1))
    def _():
        narrow = 128
        full = functools.partial(jnp.dot, precision=lax.Precision.HIGHEST,
                                 preferred_element_type=f32)
        sums = jnp.sum(jnp.abs(gram[...]), axis=0, keepdims=True)
        guess = 1.0 / jnp.max(sums, axis=1, keepdims=True)

        def start(ds, at):
            left[:, ds] = ident_part(obs, narrow, at) * guess

        each(obs, narrow, start)

        def blocks(body, carry):
            def across(ds, at, carry):
                return pieces(obs, narrow, lambda dr, ar, c: body(dr, ar, ds, at, c), carry)

            return pieces(obs, narrow, across, carry)

        def advance(carry):
            def residuals(dr, ar, ds, at, error):
                eye = iota((narrow, narrow), 0) + ar == iota((narrow, narrow), 1) + at
                residual = jnp.where(eye, 1.0, 0.0) - full(gram[dr, :], left[:, ds])
                other[dr, ds] = residual
                return error + jnp.sum(residual * residual)

            def update(dr, ar, ds, at, carry):
                spare[dr, ds] = left[dr, ds] + full(left[dr, :], other[:, ds])
                return carry

            error = blocks(residuals, jnp.float32(0.0))
            blocks(update, 0)
            left[...] = spare[...]
            return carry[0] + 1, error

        lax.while_loop(lambda c: (c[0] < 40) & jnp.logical_not(c[1] < 1e-7), advance,
                       (jnp.int32(0), jnp.float32(1.0)))
        xb[...] = left[...].astype(bf16)
        eh[...], el[...] = split2(left[...] - xb[...].astype(f32))


def innovate(val_r, var_r, scale_r, o, n, vh, vl):
    deviation = jnp.sqrt(var_r)

    def rows(ds, at):
        part = val_r + deviation * n[ds, :] - o[:, ds].T
        vh[ds, :], vl[ds, :] = split2(part * scale_r)

    each(n.shape[0], 128, rows)


def weigh(pos_c, pos_dev, x, high, middle, members):
    xh, xl = split2(x - jnp.mean(x, axis=0, keepdims=True))
    cross = nn(high[...], xh) + nn(high[...], xl) + nn(middle[...], xh)
    return taper(pos_c, pos_dev) * cross * (1.0 / (members - 1))


def columns(par_ref):
    return jnp.concatenate([par_ref[...], jnp.zeros((120, par_ref.shape[1]), f32)], axis=0).T


def own_positions(first, rows_dev, bin_rows):
    return right(first + iota((1, rows_dev), 1), shift_of(bin_rows)).astype(f32)


def first_kernel(dims, where_ref, par_ref, oa, ob, x_ref,
                 o, high, middle, xb, eh, el, vec, wh, wl, *work):
    bin_rows, nzl, ny = dims
    where = [where_ref[k] for k in range(3)]
    _, members = o.shape
    low, left, gram, other, spare, s_high, s_low, xa, ra, rb = work
    put_in_place(where, oa, ob, o, 0, 1, nzl, ny)
    pos_c = columns(par_ref)[:, 0:1]
    pos_dev = own_positions(where_ref[3], x_ref.shape[1], bin_rows)
    centre(o, high, middle, low)
    invert(par_ref.at[0:1], par_ref.at[2:3], pos_c, members, high, middle, low, left, gram, other,
           spare, s_high, s_low, xa, xb, ra, rb, eh, el, vec)
    wh[...], wl[...] = split2(weigh(pos_c, pos_dev, x_ref[...], high, middle, members))


def second_kernel(dims, where_ref, par_ref, oa, ob, na, nb, x_ref,
                  o0, high0, middle0, xb0, eh0, el0, vec0, wh0, wl0,
                  out_ref, high, middle, o, n, vh, vl, sh, sl, xb, eh, el, vec, *work):
    bin_rows, nzl, ny = dims
    where = [where_ref[k] for k in range(3)]
    obs, members = o.shape
    low, left, gram, other, spare, s_high, s_low, xa, ra, rb = work
    pos_c = columns(par_ref)[:, 4:5]
    pos_dev = own_positions(where_ref[3], x_ref.shape[1], bin_rows)
    norming = 1.0 / (members - 1)
    put_in_place(where, na, nb, n, 0, 2, nzl, ny)
    innovate(par_ref[1:2, :], par_ref[2:3, :], vec0[0:1, :], o0, n, vh, vl)

    def solve(ds, at):
        part = nn(vh[...], xb0[:, ds]) + nn(vl[...], xb0[:, ds])
        part = part + nn(vh[...], eh0[:, ds]) + nn(vh[...], el0[:, ds])
        sh[:, ds], sl[:, ds] = split2(part * vec0[0:1, ds])

    each(obs, obs // 2, solve)
    out_ref[...] = (x_ref[...] + nn(sh[...], wh0[...]) + nn(sh[...], wl0[...])
                    + nn(sl[...], wh0[...]))
    put_in_place(where, oa, ob, o, 0, 1, nzl, ny)
    put_in_place(where, na, nb, n, 1, 2, nzl, ny)
    centre(o, high, middle, low)

    def weights(ds, at):
        cross = nt(high[...], high0[ds, :]) + nt(high[...], middle0[ds, :])
        cross = cross + nt(middle[...], high0[ds, :])
        xa[:, ds], xb[:, ds] = split2(taper(pos_c, par_ref[0:1, ds]) * cross * norming)

    each(obs, obs // 2, weights)

    def update(ds, at):
        o[:, ds] = (o[:, ds] + nt(xa[...], sh[ds, :]) + nt(xa[...], sl[ds, :])
                    + nt(xb[...], sh[ds, :]))

    each(members, members // 2, update)
    centre(o, high, middle, low)
    invert(par_ref.at[4:5], par_ref.at[6:7], pos_c, members, high, middle, low, left, gram, other,
           spare, s_high, s_low, xa, xb, ra, rb, eh, el, vec)
    scale_c = column_of(vec[0:1, :])
    wh, wl = split2(weigh(pos_c, pos_dev, out_ref[...], high, middle, members) * scale_c)
    applied = nn(xb[...], wh) + nn(xb[...], wl) + nn(eh[...], wh) + nn(el[...], wh)
    wh, wl = split2(applied * scale_c)
    innovate(par_ref[5:6, :], par_ref[6:7, :], jnp.ones((1, obs), f32), o, n, vh, vl)
    out_ref[...] = out_ref[...] + nn(vh[...], wh) + nn(vh[...], wl) + nn(vl[...], wh)


def ring_gather(value, axis, size):
    parts = [value] + [
        lax.ppermute(value, axis, [(i, (i + k) % size) for i in range(size)])
        for k in range(1, size)
    ]
    return jnp.concatenate(parts, axis=0)


def on_device(state, obs_index, obs_values, obs_var, noise):
    members, rows_dev = state.shape
    batches, obs = obs_index.shape
    cols = lax.axis_size(COL)
    nx, nz, nc = (lax.axis_size(a) for a in ROW)
    nzl, ny = (lax.axis_size(a) for a in COL)
    my_col = lax.axis_index(COL)
    my_tile = lax.axis_index(ROW)
    tile_rows = rows_dev * cols
    bin_rows = tile_rows * nx * nz * nc // POSITIONS
    first = (my_tile * cols + my_col) * rows_dev
    core = lax.axis_index("core")
    noise = jnp.swapaxes(noise, 1, 2)
    slots = cols * batches * SLOTS
    unit = obs // cols // nc
    prep_dims = (tile_rows, bin_rows, cols)

    def scalars(*values):
        return jnp.stack([jnp.asarray(v, i32) for v in values])

    smem = pl.BlockSpec(memory_space=pltpu.SMEM)
    vmem = pl.BlockSpec(memory_space=pltpu.VMEM)

    def call(kernel, shapes, inputs, scratch=(), flops=0, room=16):
        return pl.pallas_call(
            kernel,
            out_shape=shapes,
            in_specs=[smem] + [vmem] * (len(inputs) - 1),
            out_specs=jax.tree.map(lambda _: vmem, shapes),
            scratch_shapes=list(scratch),
            cost_estimate=pl.CostEstimate(flops=flops, bytes_accessed=4 << 20, transcendentals=0),
            compiler_params=pltpu.CompilerParams(vmem_limit_bytes=room << 20),
        )(*inputs)

    par, noise_t = call(
        functools.partial(par_kernel, (bin_rows, tile_rows, cols)),
        (jax.ShapeDtypeStruct((4 * batches, obs), f32), jax.ShapeDtypeStruct(noise.shape, f32)),
        (scalars(0), obs_index, obs_values, obs_var, noise), flops=1 << 30)

    def exchange(turn, held):
        send = call(
            functools.partial(send_kernel, prep_dims),
            jax.ShapeDtypeStruct((slots, members), f32),
            (scalars(my_tile, first, turn), obs_index, state), flops=1 << 28)
        mine = lax.all_to_all(send.reshape(cols, batches * SLOTS, members), COL, 0, 0, tiled=True)
        mine = jnp.sum(mine, axis=0)
        mine = ring_gather(mine, "zh", nz)
        mine = ring_gather(mine, "x", nx)
        mine = ring_gather(mine, "core", nc)
        return call(
            functools.partial(place_kernel, (tile_rows, cols, (nx, nz, nc))),
            jax.ShapeDtypeStruct((batches * unit, members), f32),
            (scalars(my_col, turn, *(lax.axis_index(a) for a in ROW)), obs_index, mine, held),
            flops=1 << 28)

    tiles = obs_index[:, :, None] // tile_rows == jnp.arange(nx * nz * nc, dtype=i32)
    most = jnp.max(jnp.sum(tiles.astype(i32), axis=1))
    turns = (most + cols * SLOTS - 1) // (cols * SLOTS)
    held = lax.fori_loop(0, turns, exchange, jnp.zeros((batches * unit, members), f32))

    swap = [(0, 1), (1, 0)]
    part = noise.shape[1] // nc
    noise_half = lax.dynamic_slice_in_dim(noise_t, core * part, part, axis=1)
    na = ring_gather(noise_half.reshape(batches * part, obs), "zl", nzl)
    na, held = lax.optimization_barrier((na, held))
    na = ring_gather(na, "y", ny)
    oa, later = held[:unit], held[unit:]
    oa = ring_gather(oa, "zl", nzl)
    oa, later = lax.optimization_barrier((oa, later))
    oa = ring_gather(oa, "y", ny)
    ob = lax.ppermute(oa, "core", swap)
    la = ring_gather(later, "zl", nzl)
    la = ring_gather(la, "y", ny)
    full = (obs, members)
    wide, slim = pltpu.VMEM(full, f32), pltpu.VMEM(full, bf16)
    work = [slim] + [wide] * 4 + [slim] * 5
    where = scalars(lax.axis_index("zl"), lax.axis_index("y"), core, first)
    dims = (bin_rows, nzl, ny)
    halved = jax.ShapeDtypeStruct(full, bf16)
    weights = jax.ShapeDtypeStruct((obs, rows_dev), bf16)
    found = call(
        functools.partial(first_kernel, dims),
        (jax.ShapeDtypeStruct(full, f32), halved, halved, halved, halved, halved,
         jax.ShapeDtypeStruct((8, obs), f32), weights, weights),
        (where, par, oa, ob, state), scratch=work, flops=7 << 30, room=24)
    la, na, *found = lax.optimization_barrier((la, na, *found))
    lb = lax.ppermute(la, "core", swap)
    nb = lax.ppermute(na, "core", swap)
    return call(
        functools.partial(second_kernel, dims),
        jax.ShapeDtypeStruct(state.shape, f32),
        (where, par, la, lb, na, nb, state, *found),
        scratch=([slim] * 2 + [wide] * 2 + [slim] * 7 + [pltpu.VMEM((8, obs), f32)] + work),
        flops=12 << 30, room=30)


def solution(mesh):
    split = Mesh(mesh.devices.reshape(4, 2, 2, 4, 4), ROW_COL)
    placed = (P(None, ROW_COL), P(), P(), P(), P(None, None, COL))

    return jax.shard_map(
        on_device, mesh=split, in_specs=placed, out_specs=P(None, ROW_COL), check_vma=False
    )
```

profile of v0, /device:TPU:32, one launch (start us, length us, event | category | flops | bytes accessed | tf_op | source)
XLA Modules:
  0.0 410.5 jit_solution(17629467889985201172)
XLA Ops:
  0.7 0.9 copy-done
  1.6 2.2 shard_map.55
  3.9 1.9 collective-permute-start.7
  5.8 1.6 collective-permute-start.6
  7.3 2.8 collective-permute-start.5
  12.0 1.3 collective-permute-done.5
  13.3 37.1 %while.10 = (s32[]{:T(128)}, f32[32,512]{1,0:T(8,128)S(1)}, s32[]{:T(128)}, s32[]{:T(128)}, s32[]{:T(128)}, /*index=5*/s32[]{:T(128)}, s32[2,512]{1,0:T(2,128)S(...) while((s32[]{:T(128)}, f32[32,512]{1,0:T(8,128)S(1)}, ...), condition=%wide.region_4.5_spmd, body=%wide.region_2.4_spmd.sunk | while | flops 536940544 | bytes 11026945 | solution.py:497
  13.4 1.7 body.2
  15.1 16.4 %all_to_all.6 = f32[16,8,512]{2,1,0:T(8,128)S(1)} all-to-all(f32[16,8,512]{2,1,0:T(8,128)S(1)} %bitcast.30), channel_id=1, replica_groups=mesh['x'=4,'zh'=2,'core'=2,'zl'=4,'y'=4] {'zl','y'}, dimensions={0} | all-to-all | bytes 524288 | tf_op jit(solution)/shard_map/while/body/all_to_all | solution.py:483
  31.5 5.4 %collective-permute-start = (f32[8,512]{1,0:T(8,128)S(1)}, f32[8,512]{1,0:T(8,128)S(1)}, u32[]{:S(2)}, u32[]{:S(2)}) collective-permute-start(f32[8,512]{1,0:T(8,128)S(1)} %reduce_sum.21), channel_id=1, source_target_pairs={{0,32},{32,0},{1,33},{33,1},{2,34},{34,2},{3,35},{35,3},{4,36},{36... | collective-permute-start | bytes 49160 | tf_op jit(solution)/shard_map/while/body/ppermute | solution.py:433
  37.0 2.3 collective-permute-done
  39.3 2.8 collective-permute-start.3
  42.8 0.9 collective-permute-start.1
  43.7 4.2 %collective-permute-done.1 = f32[16,512]{1,0:T(8,128)S(1)} collective-permute-done((f32[16,512]{1,0:T(8,128)S(1)}, f32[16,512]{1,0:T(8,128)S(1)}, u32[]{:S(2)}, u32[]{:S(2)}) %collective-permute-start.1) | collective-permute-done | bytes 32800 | tf_op jit(solution)/shard_map/while/body/ppermute | solution.py:433
  48.2 1.2 collective-permute-done.4
  49.5 0.9 body.3
  50.4 1.5 collective-permute-start.10
  51.9 1.1 collective-permute-start.9
  53.0 1.7 collective-permute-start.8
  54.7 2.4 collective-permute-done.9
  57.1 2.7 collective-permute-start.13
  60.2 1.7 collective-permute-start.11
  62.5 1.9 collective-permute-start.21
  64.7 3.6 collective-permute-start.15
  68.8 5.8 %collective-permute-done.20 = f32[64,512]{1,0:T(8,128)S(1)} collective-permute-done((f32[64,512]{1,0:T(8,128)S(1)}, f32[64,512]{1,0:T(8,128)S(1)}, u32[]{:S(2)}, u32[]{:S(2)}) %collective-permute-start.20) | collective-permute-done | bytes 131104 | tf_op jit(solution)/shard_map/ppermute | solution.py:433
  74.9 1.1 collective-permute-start.18
  75.9 1.3 collective-permute-start.17
  77.3 2.4 collective-permute-start.16
  79.7 12.3 %collective-permute-done.16 = f32[64,512]{1,0:T(8,128)S(1)} collective-permute-done((f32[64,512]{1,0:T(8,128)S(1)}, f32[64,512]{1,0:T(8,128)S(1)}, u32[]{:S(2)}, u32[]{:S(2)}) %collective-permute-start.16) | collective-permute-done | bytes 131104 | tf_op jit(solution)/shard_map/ppermute | solution.py:433
  92.1 166.9 %shard_map.56 = (f32[512,512]{1,0:T(8,128)S(1)}, bf16[512,512]{1,0:T(8,128)(2,1)S(1)}, bf16[512,512]{1,0:T(8,128)(2,1)S(1)}, bf16[512,512]{1,0:T(8,128)(2,1)S(1)...) custom-call(s32[4]{0:T(128)S(1)} %pad_add_fusion.1.where_ref, ...), custom_call_target="tpu_custom_call" | custom-call | flops 7516192768 | bytes 4194304 | tf_op jit(solution)/shard_map/pallas_call | solution.py:463
  259.6 2.9 collective-permute-done.24.ob
  262.5 148.0 %shard_map.57 = f32[512,256]{1,0:T(8,128)} custom-call(s32[4]{0:T(128)S(1)} %pad_add_fusion.1.where_ref, f32[8,512]{1,0:T(8,128)S(1)} %get-tuple-element.74.par_ref, f32[256,512]{1,0:T(8,128)S(1)} %constant_dynamic-update-slice_fusion.15.oa, f32[256,512]{1,0:T(8,128)S(1)} %collective-permute-done.24.ob, f32[512,512]{1,0:T(8,128)S(1)} %pad_maximum_fusion.1.na, ...), custom_call_target="tpu_custom_call" | custom-call | flops 12884901888 | bytes 4194304 | tf_op jit(solution)/shard_map/pallas_call | solution.py:463
  (69 shorter events, 5.9 us)
Async XLA Ops:
  0.0 0.7 copy-start.3
  0.0 0.7 copy-start.2
  0.0 0.7 copy-start.1
  0.7 0.9 copy-start
  3.8 9.5 %copy-start.4 = (f32[512,256]{1,0:T(8,128)S(1)}, f32[512,256]{1,0:T(8,128)}, u32[]{:S(2)}) copy-start(f32[512,256]{1,0:T(8,128)} %x_ref.3) | copy-start | bytes 1572868
  3.9 7.6 %collective-permute-start.7 = (f32[32,512]{1,0:T(8,128)S(1)}, f32[32,512]{1,0:T(8,128)S(1)}, u32[]{:S(2)}, u32[]{:S(2)}) collective-permute-start(f32[32,512]{1,0:T(8,128)S(1)} %bitcast.32), channel_id=1, source_target_pairs={{0,12},{4,0},{8,4},{12,8},{1,13},{5,1},{9,5},{13,9},{2,14},{6,2},{... | collective-permute-start | bytes 196616 | tf_op jit(solution)/shard_map/ppermute | solution.py:433
  5.8 6.3 %collective-permute-start.6 = (f32[32,512]{1,0:T(8,128)S(1)}, f32[32,512]{1,0:T(8,128)S(1)}, u32[]{:S(2)}, u32[]{:S(2)}) collective-permute-start(f32[32,512]{1,0:T(8,128)S(1)} %bitcast.33), channel_id=1, source_target_pairs={{0,8},{4,12},{8,0},{12,4},{1,9},{5,13},{9,1},{13,5},{2,10},{6,14},... | collective-permute-start | bytes 196616 | tf_op jit(solution)/shard_map/ppermute | solution.py:433
  7.3 6.0 %collective-permute-start.5 = (f32[32,512]{1,0:T(8,128)S(1)}, f32[32,512]{1,0:T(8,128)S(1)}, u32[]{:S(2)}, u32[]{:S(2)}) collective-permute-start(f32[32,512]{1,0:T(8,128)S(1)} %bitcast.34), channel_id=1, source_target_pairs={{0,4},{4,8},{8,12},{12,0},{1,5},{5,9},{9,13},{13,1},{2,6},{6,10},{... | collective-permute-start | bytes 196616 | tf_op jit(solution)/shard_map/ppermute | solution.py:433
  31.5 7.7 %collective-permute-start = (f32[8,512]{1,0:T(8,128)S(1)}, f32[8,512]{1,0:T(8,128)S(1)}, u32[]{:S(2)}, u32[]{:S(2)}) collective-permute-start(f32[8,512]{1,0:T(8,128)S(1)} %reduce_sum.21), channel_id=1, source_target_pairs={{0,32},{32,0},{1,33},{33,1},{2,34},{34,2},{3,35},{35,3},{4,36},{36... | collective-permute-start | bytes 49160 | tf_op jit(solution)/shard_map/while/body/ppermute | solution.py:433
  39.3 8.7 %collective-permute-start.3 = (f32[16,512]{1,0:T(8,128)S(1)}, f32[16,512]{1,0:T(8,128)S(1)}, u32[]{:S(2)}, u32[]{:S(2)}) collective-permute-start(f32[16,512]{1,0:T(8,128)S(1)} %pad_maximum_fusion.5), channel_id=1, source_target_pairs={{0,192},{64,0},{128,64},{192,128},{1,193},{65,1},{129,65},{193,129... | collective-permute-start | bytes 98312 | tf_op jit(solution)/shard_map/while/body/ppermute | solution.py:433
  42.0 5.9 %collective-permute-start.2 = (f32[16,512]{1,0:T(8,128)S(1)}, f32[16,512]{1,0:T(8,128)S(1)}, u32[]{:S(2)}, u32[]{:S(2)}) collective-permute-start(f32[16,512]{1,0:T(8,128)S(1)} %pad_maximum_fusion.5), channel_id=1, source_target_pairs={{0,128},{64,192},{128,0},{192,64},{1,129},{65,193},{129,1},{193,65... | collective-permute-start | bytes 98312 | tf_op jit(solution)/shard_map/while/body/ppermute | solution.py:433
  42.8 5.1 %collective-permute-start.1 = (f32[16,512]{1,0:T(8,128)S(1)}, f32[16,512]{1,0:T(8,128)S(1)}, u32[]{:S(2)}, u32[]{:S(2)}) collective-permute-start(f32[16,512]{1,0:T(8,128)S(1)} %pad_maximum_fusion.5), channel_id=1, source_target_pairs={{0,64},{64,128},{128,192},{192,0},{1,65},{65,129},{129,193},{193,1... | collective-permute-start | bytes 98312 | tf_op jit(solution)/shard_map/while/body/ppermute | solution.py:433
  48.0 1.4 collective-permute-start.4
  50.4 4.3 %collective-permute-start.10 = (f32[16,512]{1,0:T(8,128)S(1)}, f32[16,512]{1,0:T(8,128)S(1)}, u32[]{:S(2)}, u32[]{:S(2)}) collective-permute-start(f32[16,512]{1,0:T(8,128)S(1)} %get-tuple-element.128), channel_id=1, source_target_pairs={{0,12},{4,0},{8,4},{12,8},{1,13},{5,1},{9,5},{13,9},{2,14},{6,2},{... | collective-permute-start | bytes 98312 | tf_op jit(solution)/shard_map/ppermute | solution.py:433
  51.9 5.2 %collective-permute-start.9 = (f32[16,512]{1,0:T(8,128)S(1)}, f32[16,512]{1,0:T(8,128)S(1)}, u32[]{:S(2)}, u32[]{:S(2)}) collective-permute-start(f32[16,512]{1,0:T(8,128)S(1)} %get-tuple-element.128), channel_id=1, source_target_pairs={{0,8},{4,12},{8,0},{12,4},{1,9},{5,13},{9,1},{13,5},{2,10},{6,14},... | collective-permute-start | bytes 98312 | tf_op jit(solution)/shard_map/ppermute | solution.py:433
  53.0 4.1 collective-permute-start.8
  57.1 7.6 %collective-permute-start.13 = (f32[16,512]{1,0:T(8,128)S(1)}, f32[16,512]{1,0:T(8,128)S(1)}, u32[]{:S(2)}, u32[]{:S(2)}) collective-permute-start(f32[16,512]{1,0:T(8,128)S(1)} %get-tuple-element.78), channel_id=1, source_target_pairs={{0,12},{4,0},{8,4},{12,8},{1,13},{5,1},{9,5},{13,9},{2,14},{6,2},{... | collective-permute-start | bytes 98312 | tf_op jit(solution)/shard_map/ppermute | solution.py:433
  59.8 4.9 %collective-permute-start.12 = (f32[16,512]{1,0:T(8,128)S(1)}, f32[16,512]{1,0:T(8,128)S(1)}, u32[]{:S(2)}, u32[]{:S(2)}) collective-permute-start(f32[16,512]{1,0:T(8,128)S(1)} %get-tuple-element.78), channel_id=1, source_target_pairs={{0,8},{4,12},{8,0},{12,4},{1,9},{5,13},{9,1},{13,5},{2,10},{6,14},... | collective-permute-start | bytes 98312 | tf_op jit(solution)/shard_map/ppermute | solution.py:433
  60.2 4.3 %collective-permute-start.11 = (f32[16,512]{1,0:T(8,128)S(1)}, f32[16,512]{1,0:T(8,128)S(1)}, u32[]{:S(2)}, u32[]{:S(2)}) collective-permute-start(f32[16,512]{1,0:T(8,128)S(1)} %get-tuple-element.78), channel_id=1, source_target_pairs={{0,4},{4,8},{8,12},{12,0},{1,5},{5,9},{9,13},{13,1},{2,6},{6,10},{... | collective-permute-start | bytes 98312 | tf_op jit(solution)/shard_map/ppermute | solution.py:433
  61.9 12.8 %collective-permute-start.22 = (f32[64,512]{1,0:T(8,128)S(1)}, f32[64,512]{1,0:T(8,128)S(1)}, u32[]{:S(2)}, u32[]{:S(2)}) collective-permute-start(f32[64,512]{1,0:T(8,128)S(1)} %pad_maximum_fusion.3), channel_id=1, source_target_pairs={{0,3},{1,0},{2,1},{3,2},{4,7},{5,4},{6,5},{7,6},{8,11},{9,8},{10,9... | collective-permute-start | bytes 393224 | tf_op jit(solution)/shard_map/ppermute | solution.py:433
  62.5 12.1 %collective-permute-start.21 = (f32[64,512]{1,0:T(8,128)S(1)}, f32[64,512]{1,0:T(8,128)S(1)}, u32[]{:S(2)}, u32[]{:S(2)}) collective-permute-start(f32[64,512]{1,0:T(8,128)S(1)} %pad_maximum_fusion.3), channel_id=1, source_target_pairs={{0,2},{1,3},{2,0},{3,1},{4,6},{5,7},{6,4},{7,5},{8,10},{9,11},{10,... | collective-permute-start | bytes 393224 | tf_op jit(solution)/shard_map/ppermute | solution.py:433
  64.5 10.1 %collective-permute-start.20 = (f32[64,512]{1,0:T(8,128)S(1)}, f32[64,512]{1,0:T(8,128)S(1)}, u32[]{:S(2)}, u32[]{:S(2)}) collective-permute-start(f32[64,512]{1,0:T(8,128)S(1)} %pad_maximum_fusion.3), channel_id=1, source_target_pairs={{0,1},{1,2},{2,3},{3,0},{4,5},{5,6},{6,7},{7,4},{8,9},{9,10},{10,1... | collective-permute-start | bytes 393224 | tf_op jit(solution)/shard_map/ppermute | solution.py:433
  64.7 11.2 %collective-permute-start.15 = (f32[64,512]{1,0:T(8,128)S(1)}, f32[64,512]{1,0:T(8,128)S(1)}, u32[]{:S(2)}, u32[]{:S(2)}) collective-permute-start(f32[64,512]{1,0:T(8,128)S(1)} %get-tuple-element.129), channel_id=1, source_target_pairs={{0,2},{1,3},{2,0},{3,1},{4,6},{5,7},{6,4},{7,5},{8,10},{9,11},{10,... | collective-permute-start | bytes 393224 | tf_op jit(solution)/shard_map/ppermute | solution.py:433
  68.3 9.0 %collective-permute-start.14 = (f32[64,512]{1,0:T(8,128)S(1)}, f32[64,512]{1,0:T(8,128)S(1)}, u32[]{:S(2)}, u32[]{:S(2)}) collective-permute-start(f32[64,512]{1,0:T(8,128)S(1)} %get-tuple-element.129), channel_id=1, source_target_pairs={{0,1},{1,2},{2,3},{3,0},{4,5},{5,6},{6,7},{7,4},{8,9},{9,10},{10,1... | collective-permute-start | bytes 393224 | tf_op jit(solution)/shard_map/ppermute | solution.py:433
  74.6 17.5 %collective-permute-start.23 = (f32[256,512]{1,0:T(8,128)S(1)}, f32[256,512]{1,0:T(8,128)S(1)}, u32[]{:S(2)}, u32[]{:S(2)}) collective-permute-start(f32[256,512]{1,0:T(8,128)S(1)} %constant_dynamic-update-slice_fusion.22.oa), channel_id=1, source_target_pairs={{0,16},{16,0},{1,17},{17,1},{2,18},{18,2},{3,19},{19,3},{4,20},{20... | collective-permute-start | bytes 1572872 | tf_op jit(solution)/shard_map/ppermute | solution.py:509
  74.8 17.2 %collective-permute-start.19 = (f32[128,512]{1,0:T(8,128)S(1)}, f32[128,512]{1,0:T(8,128)S(1)}, u32[]{:S(2)}, u32[]{:S(2)}) collective-permute-start(f32[128,512]{1,0:T(8,128)S(1)} %pad_maximum_fusion.2), channel_id=1, source_target_pairs={{0,3},{1,0},{2,1},{3,2},{4,7},{5,4},{6,5},{7,6},{8,11},{9,8},{10,9... | collective-permute-start | bytes 786440 | tf_op jit(solution)/shard_map/ppermute | solution.py:433
  74.9 17.2 %collective-permute-start.18 = (f32[128,512]{1,0:T(8,128)S(1)}, f32[128,512]{1,0:T(8,128)S(1)}, u32[]{:S(2)}, u32[]{:S(2)}) collective-permute-start(f32[128,512]{1,0:T(8,128)S(1)} %pad_maximum_fusion.2), channel_id=1, source_target_pairs={{0,2},{1,3},{2,0},{3,1},{4,6},{5,7},{6,4},{7,5},{8,10},{9,11},{10,... | collective-permute-start | bytes 786440 | tf_op jit(solution)/shard_map/ppermute | solution.py:433
  75.9 16.1 %collective-permute-start.17 = (f32[128,512]{1,0:T(8,128)S(1)}, f32[128,512]{1,0:T(8,128)S(1)}, u32[]{:S(2)}, u32[]{:S(2)}) collective-permute-start(f32[128,512]{1,0:T(8,128)S(1)} %pad_maximum_fusion.2), channel_id=1, source_target_pairs={{0,1},{1,2},{2,3},{3,0},{4,5},{5,6},{6,7},{7,4},{8,9},{9,10},{10,1... | collective-permute-start | bytes 786440 | tf_op jit(solution)/shard_map/ppermute | solution.py:433
  77.3 14.7 %collective-permute-start.16 = (f32[64,512]{1,0:T(8,128)S(1)}, f32[64,512]{1,0:T(8,128)S(1)}, u32[]{:S(2)}, u32[]{:S(2)}) collective-permute-start(f32[64,512]{1,0:T(8,128)S(1)} %get-tuple-element.129), channel_id=1, source_target_pairs={{0,3},{1,0},{2,1},{3,2},{4,7},{5,4},{6,5},{7,6},{8,11},{9,8},{10,9... | collective-permute-start | bytes 393224 | tf_op jit(solution)/shard_map/ppermute | solution.py:433
  259.0 3.5 collective-permute-start.25
  259.1 3.4 collective-permute-start.24
where the time goes:
time: 411 us
  Pallas kernels  320 us (78%)
  starting transfers between devices  37.6 us (9%)
  waiting for transfers between devices  32.9 us (8%)
  blocking collectives  16.4 us (4%)
    pallas_call x5, Pallas kernels, call(): pl.pallas_call(kernel, out_shape=shapes, in_specs=[smem] + [vmem] * (len(...  320 us
    ppermute x23, starting transfers between devices, ring_gather(): lax.ppermute(value, axis, [(i, (i + k) % size) for i in range(size)])  36.9 us
    ppermute x23, waiting for transfers between devices, ring_gather(): lax.ppermute(value, axis, [(i, (i + k) % size) for i in range(size)])  30 us
    all_to_all x1, blocking collectives, exchange(): lax.all_to_all(send.reshape(cols, batches * SLOTS, members), COL, 0, 0, t...  16.4 us
  transfers between devices with their start and end apart: 26, of which 9 were waited for; matrix products, arithmetic and copies ran while one was open for 0% of the time, Pallas kernels for 0%

commit v1 on v0

--- a/solution.py
+++ b/solution.py
@@ -181,11 +181,8 @@
 
 
 def each(size, width, body):
-    def step(ds, at, carry):
-        body(ds, at)
-        return carry
-
-    pieces(size, width, step)
+    for at in range(0, size, width):
+        body(slice(at, at + width), at)
 
 
 def eye_part(obs, width, at):
@@ -208,7 +205,7 @@
 def invert(pos_r, var_r, pos_c, members, high, middle, low, left, gram, other, spare, s_high, s_low,
            xa, xb, ra, rb, eh, el, vec):
     obs = gram.shape[0]
-    width = obs // 2
+    width = obs
     norming = 1.0 / (members - 1)
 
     def cross_terms(ds, at):
@@ -365,44 +362,30 @@
     return right(first + iota((1, rows_dev), 1), shift_of(bin_rows)).astype(f32)
 
 
-def first_kernel(dims, where_ref, par_ref, oa, ob, x_ref,
-                 o, high, middle, xb, eh, el, vec, wh, wl, *work):
-    bin_rows, nzl, ny = dims
-    where = [where_ref[k] for k in range(3)]
-    _, members = o.shape
-    low, left, gram, other, spare, s_high, s_low, xa, ra, rb = work
-    put_in_place(where, oa, ob, o, 0, 1, nzl, ny)
-    pos_c = columns(par_ref)[:, 0:1]
-    pos_dev = own_positions(where_ref[3], x_ref.shape[1], bin_rows)
-    centre(o, high, middle, low)
-    invert(par_ref.at[0:1], par_ref.at[2:3], pos_c, members, high, middle, low, left, gram, other,
-           spare, s_high, s_low, xa, xb, ra, rb, eh, el, vec)
-    wh[...], wl[...] = split2(weigh(pos_c, pos_dev, x_ref[...], high, middle, members))
-
-
-def second_kernel(dims, where_ref, par_ref, oa, ob, na, nb, x_ref,
-                  o0, high0, middle0, xb0, eh0, el0, vec0, wh0, wl0,
-                  out_ref, high, middle, o, n, vh, vl, sh, sl, xb, eh, el, vec, *work):
+def main_kernel(dims, where_ref, par_ref, oa, ob, na, nb, x_ref, out_ref,
+                high0, middle0, high, middle, o0, o, n, vh, vl, sh, sl, xb, eh, el, vec, *work):
     bin_rows, nzl, ny = dims
     where = [where_ref[k] for k in range(3)]
     obs, members = o.shape
     low, left, gram, other, spare, s_high, s_low, xa, ra, rb = work
-    pos_c = columns(par_ref)[:, 4:5]
+    cols_par = columns(par_ref)
     pos_dev = own_positions(where_ref[3], x_ref.shape[1], bin_rows)
     norming = 1.0 / (members - 1)
+    put_in_place(where, oa, ob, o0, 0, 2, nzl, ny)
     put_in_place(where, na, nb, n, 0, 2, nzl, ny)
-    innovate(par_ref[1:2, :], par_ref[2:3, :], vec0[0:1, :], o0, n, vh, vl)
-
-    def solve(ds, at):
-        part = nn(vh[...], xb0[:, ds]) + nn(vl[...], xb0[:, ds])
-        part = part + nn(vh[...], eh0[:, ds]) + nn(vh[...], el0[:, ds])
-        sh[:, ds], sl[:, ds] = split2(part * vec0[0:1, ds])
-
-    each(obs, obs // 2, solve)
-    out_ref[...] = (x_ref[...] + nn(sh[...], wh0[...]) + nn(sh[...], wl0[...])
-                    + nn(sl[...], wh0[...]))
-    put_in_place(where, oa, ob, o, 0, 1, nzl, ny)
+    pos_c = cols_par[:, 0:1]
+    centre(o0, high0, middle0, low)
+    invert(par_ref.at[0:1], par_ref.at[2:3], pos_c, members, high0, middle0, low, left, gram,
+           other, spare, s_high, s_low, xa, xb, ra, rb, eh, el, vec)
+    innovate(par_ref[1:2, :], par_ref[2:3, :], vec[0:1, :], o0, n, vh, vl)
+    solved = nn(vh[...], xb[...]) + nn(vl[...], xb[...]) + nn(vh[...], eh[...])
+    solved = solved + nn(vh[...], el[...])
+    sh[...], sl[...] = split2(solved * vec[0:1, :])
+    wh, wl = split2(weigh(pos_c, pos_dev, x_ref[...], high0, middle0, members))
+    out_ref[...] = x_ref[...] + nn(sh[...], wh) + nn(sh[...], wl) + nn(sl[...], wh)
+    put_in_place(where, oa, ob, o, 1, 2, nzl, ny)
     put_in_place(where, na, nb, n, 1, 2, nzl, ny)
+    pos_c = cols_par[:, 4:5]
     centre(o, high, middle, low)
 
     def weights(ds, at):
@@ -410,13 +393,13 @@
         cross = cross + nt(middle[...], high0[ds, :])
         xa[:, ds], xb[:, ds] = split2(taper(pos_c, par_ref[0:1, ds]) * cross * norming)
 
-    each(obs, obs // 2, weights)
+    each(obs, obs, weights)
 
     def update(ds, at):
         o[:, ds] = (o[:, ds] + nt(xa[...], sh[ds, :]) + nt(xa[...], sl[ds, :])
                     + nt(xb[...], sh[ds, :]))
 
-    each(members, members // 2, update)
+    each(members, members, update)
     centre(o, high, middle, low)
     invert(par_ref.at[4:5], par_ref.at[6:7], pos_c, members, high, middle, low, left, gram, other,
            spare, s_high, s_low, xa, xb, ra, rb, eh, el, vec)
@@ -502,34 +485,20 @@
     na = ring_gather(noise_half.reshape(batches * part, obs), "zl", nzl)
     na, held = lax.optimization_barrier((na, held))
     na = ring_gather(na, "y", ny)
-    oa, later = held[:unit], held[unit:]
-    oa = ring_gather(oa, "zl", nzl)
-    oa, later = lax.optimization_barrier((oa, later))
+    oa = ring_gather(held, "zl", nzl)
     oa = ring_gather(oa, "y", ny)
     ob = lax.ppermute(oa, "core", swap)
-    la = ring_gather(later, "zl", nzl)
-    la = ring_gather(la, "y", ny)
+    nb = lax.ppermute(na, "core", swap)
     full = (obs, members)
     wide, slim = pltpu.VMEM(full, f32), pltpu.VMEM(full, bf16)
-    work = [slim] + [wide] * 4 + [slim] * 5
     where = scalars(lax.axis_index("zl"), lax.axis_index("y"), core, first)
-    dims = (bin_rows, nzl, ny)
-    halved = jax.ShapeDtypeStruct(full, bf16)
-    weights = jax.ShapeDtypeStruct((obs, rows_dev), bf16)
-    found = call(
-        functools.partial(first_kernel, dims),
-        (jax.ShapeDtypeStruct(full, f32), halved, halved, halved, halved, halved,
-         jax.ShapeDtypeStruct((8, obs), f32), weights, weights),
-        (where, par, oa, ob, state), scratch=work, flops=7 << 30, room=24)
-    la, na, *found = lax.optimization_barrier((la, na, *found))
-    lb = lax.ppermute(la, "core", swap)
-    nb = lax.ppermute(na, "core", swap)
     return call(
-        functools.partial(second_kernel, dims),
+        functools.partial(main_kernel, (bin_rows, nzl, ny)),
         jax.ShapeDtypeStruct(state.shape, f32),
-        (where, par, la, lb, na, nb, state, *found),
-        scratch=([slim] * 2 + [wide] * 2 + [slim] * 7 + [pltpu.VMEM((8, obs), f32)] + work),
-        flops=12 << 30, room=30)
+        (where, par, oa, ob, na, nb, state),
+        scratch=([slim] * 4 + [wide] * 3 + [slim] * 7 + [pltpu.VMEM((8, obs), f32)]
+                 + [slim] + [wide] * 4 + [slim] * 5),
+        flops=20 << 30, room=32)
 
 
 def solution(mesh):

time: 411 us -> 390 us (0.949)
  Pallas kernels: 320 us -> 309 us
  starting transfers between devices: 37.6 us -> 28.3 us
    pallas_call x5 -> x4, Pallas kernels: 320 us -> 309 us  [call(): pl.pallas_call(kernel, out_shape=shapes, in_specs=[smem] + [vmem] * (len(...]
    ppermute x23 -> x17, starting transfers between devices: 36.9 us -> 28.1 us  [ring_gather(): lax.ppermute(value, axis, [(i, (i + k) % size) for i in range(size)])]
    ppermute x23 -> x17, waiting for transfers between devices: 30 us -> 27.1 us  [ring_gather(): lax.ppermute(value, axis, [(i, (i + k) % size) for i in range(size)])]
  transfers between devices with their start and end apart: 26 -> 19, of which waited for: 9 -> 12; matrix products, arithmetic and copies ran while one was open for 0% -> 0% of each run, Pallas kernels for 0% -> 0%
where the time goes in v1:
time: 390 us; the launch traced here: 387 us
  Pallas kernels  309 us (79%)
  waiting for transfers between devices  29.7 us (8%)
  starting transfers between devices  28.3 us (7%)
  blocking collectives  16.4 us (4%)
    pallas_call x4, Pallas kernels, call(): pl.pallas_call(kernel, out_shape=shapes, in_specs=[smem] + [vmem] * (len(...  309 us
    ppermute x17, starting transfers between devices, ring_gather(): lax.ppermute(value, axis, [(i, (i + k) % size) for i in range(size)])  28.1 us
    ppermute x17, waiting for transfers between devices, ring_gather(): lax.ppermute(value, axis, [(i, (i + k) % size) for i in range(size)])  27.1 us
    all_to_all x1, blocking collectives, exchange(): lax.all_to_all(send.reshape(cols, batches * SLOTS, members), COL, 0, 0, t...  16.4 us
  transfers between devices with their start and end apart: 19, of which 12 were waited for; matrix products, arithmetic and copies ran while one was open for 0% of the time, Pallas kernels for 0%

profile of v1, /device:TPU:32, one launch (start us, length us, event | category | flops | bytes accessed | tf_op | source)
XLA Modules:
  0.0 386.9 jit_solution(12247827558467413065)
XLA Ops:
  0.0 0.7 copy-done.3
  0.7 0.9 copy-done
  1.6 2.2 shard_map.55
  3.9 1.9 collective-permute-start.7
  5.8 1.6 collective-permute-start.6
  7.3 2.8 collective-permute-start.5
  10.3 0.6 reduce_max.9
  12.0 1.3 collective-permute-done.5
  13.3 36.4 %while.10 = (s32[]{:T(128)}, f32[32,512]{1,0:T(8,128)S(1)}, s32[]{:T(128)}, s32[]{:T(128)}, s32[]{:T(128)}, /*index=5*/s32[]{:T(128)}, s32[2,512]{1,0:T(2,128)S(...) while((s32[]{:T(128)}, f32[32,512]{1,0:T(8,128)S(1)}, ...), condition=%wide.region_4.5_spmd, body=%wide.region_2.4_spmd.sunk | while | flops 536940544 | bytes 11026945 | solution.py:480
  13.4 1.7 body.2
  15.1 16.4 %all_to_all.6 = f32[16,8,512]{2,1,0:T(8,128)S(1)} all-to-all(f32[16,8,512]{2,1,0:T(8,128)S(1)} %bitcast.30), channel_id=1, replica_groups=mesh['x'=4,'zh'=2,'core'=2,'zl'=4,'y'=4] {'zl','y'}, dimensions={0} | all-to-all | bytes 524288 | tf_op jit(solution)/shard_map/while/body/all_to_all | solution.py:466
  31.5 5.4 %collective-permute-start = (f32[8,512]{1,0:T(8,128)S(1)}, f32[8,512]{1,0:T(8,128)S(1)}, u32[]{:S(2)}, u32[]{:S(2)}) collective-permute-start(f32[8,512]{1,0:T(8,128)S(1)} %reduce_sum.21), channel_id=1, source_target_pairs={{0,32},{32,0},{1,33},{33,1},{2,34},{34,2},{3,35},{35,3},{4,36},{36... | collective-permute-start | bytes 49160 | tf_op jit(solution)/shard_map/while/body/ppermute | solution.py:416
  37.0 2.3 collective-permute-done
  39.3 1.5 collective-permute-start.1
  40.8 2.7 collective-permute-start.2
  43.5 1.4 collective-permute-start.3
  44.9 1.2 collective-permute-done.2
  46.2 1.2 collective-permute-done.3
  47.5 1.2 collective-permute-done.4
  48.8 0.9 body.3
  49.7 1.1 collective-permute-start.8
  50.8 2.8 collective-permute-start.9
  53.6 0.6 collective-permute-start.15
  54.2 1.6 collective-permute-start.16
  55.8 2.0 collective-permute-start.17
  57.9 1.4 collective-permute-done.10
  59.8 2.0 collective-permute-start.12
  61.9 7.6 %collective-permute-done.15 = f32[128,512]{1,0:T(8,128)S(1)} collective-permute-done((f32[128,512]{1,0:T(8,128)S(1)}, f32[128,512]{1,0:T(8,128)S(1)}, u32[]{:S(2)}, u32[]{:S(2)}) %collective-permute-start.15) | collective-permute-done | bytes 262176 | tf_op jit(solution)/shard_map/ppermute | solution.py:416
  69.6 1.0 collective-permute-done.17
  70.7 8.8 %collective-permute-done.11 = f32[128,512]{1,0:T(8,128)S(1)} collective-permute-done((f32[128,512]{1,0:T(8,128)S(1)}, f32[128,512]{1,0:T(8,128)S(1)}, u32[]{:S(2)}, u32[]{:S(2)}) %collective-permute-start.11) | collective-permute-done | bytes 262176 | tf_op jit(solution)/shard_map/ppermute | solution.py:416
  80.4 2.6 collective-permute-done.14.ob
  82.9 304.0 %shard_map.56 = f32[512,256]{1,0:T(8,128)} custom-call(s32[4]{0:T(128)S(1)} %pad_add_fusion.1.where_ref, f32[8,512]{1,0:T(8,128)S(1)} %get-tuple-element.52.par_ref, f32[512,512]{1,0:T(8,128)S(1)} %constant_dynamic-update-slice_fusion.15.oa, f32[512,512]{1,0:T(8,128)S(1)} %collective-permute-done.14.ob, ...), custom_call_target="tpu_custom_call" | custom-call | flops 21474836480 | bytes 4194304 | tf_op jit(solution)/shard_map/pallas_call | solution.py:446
  (51 shorter events, 2.5 us)
Async XLA Ops:
  0.0 0.7 copy-start.3
  0.0 0.7 copy-start.2
  0.0 0.7 copy-start.1
  0.7 0.9 copy-start
  3.8 9.5 %copy-start.4 = (f32[512,256]{1,0:T(8,128)S(1)}, f32[512,256]{1,0:T(8,128)}, u32[]{:S(2)}) copy-start(f32[512,256]{1,0:T(8,128)} %x_ref.1) | copy-start | bytes 1572868
  3.9 7.7 %collective-permute-start.7 = (f32[32,512]{1,0:T(8,128)S(1)}, f32[32,512]{1,0:T(8,128)S(1)}, u32[]{:S(2)}, u32[]{:S(2)}) collective-permute-start(f32[32,512]{1,0:T(8,128)S(1)} %bitcast.32), channel_id=1, source_target_pairs={{0,12},{4,0},{8,4},{12,8},{1,13},{5,1},{9,5},{13,9},{2,14},{6,2},{... | collective-permute-start | bytes 196616 | tf_op jit(solution)/shard_map/ppermute | solution.py:416
  5.8 6.3 %collective-permute-start.6 = (f32[32,512]{1,0:T(8,128)S(1)}, f32[32,512]{1,0:T(8,128)S(1)}, u32[]{:S(2)}, u32[]{:S(2)}) collective-permute-start(f32[32,512]{1,0:T(8,128)S(1)} %bitcast.33), channel_id=1, source_target_pairs={{0,8},{4,12},{8,0},{12,4},{1,9},{5,13},{9,1},{13,5},{2,10},{6,14},... | collective-permute-start | bytes 196616 | tf_op jit(solution)/shard_map/ppermute | solution.py:416
  7.3 6.0 %collective-permute-start.5 = (f32[32,512]{1,0:T(8,128)S(1)}, f32[32,512]{1,0:T(8,128)S(1)}, u32[]{:S(2)}, u32[]{:S(2)}) collective-permute-start(f32[32,512]{1,0:T(8,128)S(1)} %bitcast.34), channel_id=1, source_target_pairs={{0,4},{4,8},{8,12},{12,0},{1,5},{5,9},{9,13},{13,1},{2,6},{6,10},{... | collective-permute-start | bytes 196616 | tf_op jit(solution)/shard_map/ppermute | solution.py:416
  31.5 7.7 %collective-permute-start = (f32[8,512]{1,0:T(8,128)S(1)}, f32[8,512]{1,0:T(8,128)S(1)}, u32[]{:S(2)}, u32[]{:S(2)}) collective-permute-start(f32[8,512]{1,0:T(8,128)S(1)} %reduce_sum.21), channel_id=1, source_target_pairs={{0,32},{32,0},{1,33},{33,1},{2,34},{34,2},{3,35},{35,3},{4,36},{36... | collective-permute-start | bytes 49160 | tf_op jit(solution)/shard_map/while/body/ppermute | solution.py:416
  39.3 5.7 %collective-permute-start.1 = (f32[16,512]{1,0:T(8,128)S(1)}, f32[16,512]{1,0:T(8,128)S(1)}, u32[]{:S(2)}, u32[]{:S(2)}) collective-permute-start(f32[16,512]{1,0:T(8,128)S(1)} %pad_maximum_fusion.3), channel_id=1, source_target_pairs={{0,64},{64,128},{128,192},{192,0},{1,65},{65,129},{129,193},{193,1... | collective-permute-start | bytes 98312 | tf_op jit(solution)/shard_map/while/body/ppermute | solution.py:416
  40.8 5.4 %collective-permute-start.2 = (f32[16,512]{1,0:T(8,128)S(1)}, f32[16,512]{1,0:T(8,128)S(1)}, u32[]{:S(2)}, u32[]{:S(2)}) collective-permute-start(f32[16,512]{1,0:T(8,128)S(1)} %pad_maximum_fusion.3), channel_id=1, source_target_pairs={{0,128},{64,192},{128,0},{192,64},{1,129},{65,193},{129,1},{193,65... | collective-permute-start | bytes 98312 | tf_op jit(solution)/shard_map/while/body/ppermute | solution.py:416
  43.5 3.9 %collective-permute-start.3 = (f32[16,512]{1,0:T(8,128)S(1)}, f32[16,512]{1,0:T(8,128)S(1)}, u32[]{:S(2)}, u32[]{:S(2)}) collective-permute-start(f32[16,512]{1,0:T(8,128)S(1)} %pad_maximum_fusion.3), channel_id=1, source_target_pairs={{0,192},{64,0},{128,64},{192,128},{1,193},{65,1},{129,65},{193,129... | collective-permute-start | bytes 98312 | tf_op jit(solution)/shard_map/while/body/ppermute | solution.py:416
  47.4 1.3 collective-permute-start.4
  49.7 6.1 %collective-permute-start.8 = (f32[32,512]{1,0:T(8,128)S(1)}, f32[32,512]{1,0:T(8,128)S(1)}, u32[]{:S(2)}, u32[]{:S(2)}) collective-permute-start(f32[32,512]{1,0:T(8,128)S(1)} %get-tuple-element.55), channel_id=1, source_target_pairs={{0,4},{4,8},{8,12},{12,0},{1,5},{5,9},{9,13},{13,1},{2,6},{6,10},{... | collective-permute-start | bytes 196616 | tf_op jit(solution)/shard_map/ppermute | solution.py:416
  50.8 7.1 %collective-permute-start.9 = (f32[32,512]{1,0:T(8,128)S(1)}, f32[32,512]{1,0:T(8,128)S(1)}, u32[]{:S(2)}, u32[]{:S(2)}) collective-permute-start(f32[32,512]{1,0:T(8,128)S(1)} %get-tuple-element.55), channel_id=1, source_target_pairs={{0,8},{4,12},{8,0},{12,4},{1,9},{5,13},{9,1},{13,5},{2,10},{6,14},... | collective-permute-start | bytes 196616 | tf_op jit(solution)/shard_map/ppermute | solution.py:416
  53.5 5.7 %collective-permute-start.10 = (f32[32,512]{1,0:T(8,128)S(1)}, f32[32,512]{1,0:T(8,128)S(1)}, u32[]{:S(2)}, u32[]{:S(2)}) collective-permute-start(f32[32,512]{1,0:T(8,128)S(1)} %get-tuple-element.55), channel_id=1, source_target_pairs={{0,12},{4,0},{8,4},{12,8},{1,13},{5,1},{9,5},{13,9},{2,14},{6,2},{... | collective-permute-start | bytes 196616 | tf_op jit(solution)/shard_map/ppermute | solution.py:416
  53.6 15.9 %collective-permute-start.15 = (f32[128,512]{1,0:T(8,128)S(1)}, f32[128,512]{1,0:T(8,128)S(1)}, u32[]{:S(2)}, u32[]{:S(2)}) collective-permute-start(f32[128,512]{1,0:T(8,128)S(1)} %pad_maximum_fusion.1), channel_id=1, source_target_pairs={{0,1},{1,2},{2,3},{3,0},{4,5},{5,6},{6,7},{7,4},{8,9},{9,10},{10,1... | collective-permute-start | bytes 786440 | tf_op jit(solution)/shard_map/ppermute | solution.py:416
  54.2 15.3 %collective-permute-start.16 = (f32[128,512]{1,0:T(8,128)S(1)}, f32[128,512]{1,0:T(8,128)S(1)}, u32[]{:S(2)}, u32[]{:S(2)}) collective-permute-start(f32[128,512]{1,0:T(8,128)S(1)} %pad_maximum_fusion.1), channel_id=1, source_target_pairs={{0,2},{1,3},{2,0},{3,1},{4,6},{5,7},{6,4},{7,5},{8,10},{9,11},{10,... | collective-permute-start | bytes 786440 | tf_op jit(solution)/shard_map/ppermute | solution.py:416
  55.8 14.7 %collective-permute-start.17 = (f32[128,512]{1,0:T(8,128)S(1)}, f32[128,512]{1,0:T(8,128)S(1)}, u32[]{:S(2)}, u32[]{:S(2)}) collective-permute-start(f32[128,512]{1,0:T(8,128)S(1)} %pad_maximum_fusion.1), channel_id=1, source_target_pairs={{0,3},{1,0},{2,1},{3,2},{4,7},{5,4},{6,5},{7,6},{8,11},{9,8},{10,9... | collective-permute-start | bytes 786440 | tf_op jit(solution)/shard_map/ppermute | solution.py:416
  59.3 20.2 %collective-permute-start.11 = (f32[128,512]{1,0:T(8,128)S(1)}, f32[128,512]{1,0:T(8,128)S(1)}, u32[]{:S(2)}, u32[]{:S(2)}) collective-permute-start(f32[128,512]{1,0:T(8,128)S(1)} %get-tuple-element.83), channel_id=1, source_target_pairs={{0,1},{1,2},{2,3},{3,0},{4,5},{5,6},{6,7},{7,4},{8,9},{9,10},{10,1... | collective-permute-start | bytes 786440 | tf_op jit(solution)/shard_map/ppermute | solution.py:416
  59.8 19.7 %collective-permute-start.12 = (f32[128,512]{1,0:T(8,128)S(1)}, f32[128,512]{1,0:T(8,128)S(1)}, u32[]{:S(2)}, u32[]{:S(2)}) collective-permute-start(f32[128,512]{1,0:T(8,128)S(1)} %get-tuple-element.83), channel_id=1, source_target_pairs={{0,2},{1,3},{2,0},{3,1},{4,6},{5,7},{6,4},{7,5},{8,10},{9,11},{10,... | collective-permute-start | bytes 786440 | tf_op jit(solution)/shard_map/ppermute | solution.py:416
  69.5 10.7 %collective-permute-start.13 = (f32[128,512]{1,0:T(8,128)S(1)}, f32[128,512]{1,0:T(8,128)S(1)}, u32[]{:S(2)}, u32[]{:S(2)}) collective-permute-start(f32[128,512]{1,0:T(8,128)S(1)} %get-tuple-element.83), channel_id=1, source_target_pairs={{0,3},{1,0},{2,1},{3,2},{4,7},{5,4},{6,5},{7,6},{8,11},{9,8},{10,9... | collective-permute-start | bytes 786440 | tf_op jit(solution)/shard_map/ppermute | solution.py:416
  70.6 9.8 %collective-permute-start.18 = (f32[512,512]{1,0:T(8,128)S(1)}, f32[512,512]{1,0:T(8,128)S(1)}, u32[]{:S(2)}, u32[]{:S(2)}) collective-permute-start(f32[512,512]{1,0:T(8,128)S(1)} %constant_dynamic-update-slice_fusion.22.na), channel_id=1, source_target_pairs={{0,16},{16,0},{1,17},{17,1},{2,18},{18,2},{3,19},{19,3},{4,20},{20... | collective-permute-start | bytes 3145736 | tf_op jit(solution)/shard_map/ppermute | solution.py:491
  80.2 2.7 collective-permute-start.14

commit v2 on v1

--- a/solution.py
+++ b/solution.py
@@ -55,11 +55,6 @@
     return nt(hot, high) + nt(hot, middle) + nt(hot, low)
 
 
-def exact_tn(x, hot):
-    high, middle, low = split3(x)
-    return nt(high, hot) + nt(middle, hot) + nt(low, hot)
-
-
 def column_of(row):
     return jnp.broadcast_to(row, (128, row.shape[1])).T[:, 0:1]
 
@@ -74,7 +69,7 @@
 
 
 def right(value, bits):
-    return lax.shift_right_logical(value, jnp.full(value.shape, bits, i32))
+    return lax.shift_right_logical(value, jnp.full(jnp.shape(value), bits, i32))
 
 
 def order_of(rows, tile_rows, obs):
@@ -95,16 +90,19 @@
         hot = one_hot(iota((obs, obs), 0) == placed)
         par = jnp.concatenate(
             [right(rows, shift_of(bin_rows)).astype(f32), values_ref[b:b + 1, :],
-             var_ref[b:b + 1, :], jnp.zeros((5, obs), f32)], axis=0)
-        par_ref[4 * b:4 * b + 4, :] = exact_tn(par, hot)[0:4]
-        noise_out_ref[b] = exact_tn(noise_ref[b], hot)
+             var_ref[b:b + 1, :], jnp.zeros((13, obs), f32), noise_ref[b]], axis=0)
+        count = par.shape[0]
+        moved = nt(jnp.concatenate(split3(par), axis=0), hot)
+        moved = moved[0:count] + moved[count:2 * count] + moved[2 * count:]
+        par_ref[4 * b:4 * b + 4, :] = moved[0:4]
+        noise_out_ref[b] = moved[16:]
 
 
 def send_kernel(dims, where_ref, index_ref, state_ref, send_ref):
     tile_rows, _, cols = dims
     _, rows_dev = state_ref.shape
     batches, obs = index_ref.shape
-    my_tile, first, turn = where_ref[0], where_ref[1], where_ref[2]
+    my_tile, first = where_ref[0], where_ref[1]
     slots = send_ref.shape[0]
     per_col = slots // cols
     pick = jnp.zeros((slots, rows_dev), f32)
@@ -114,26 +112,50 @@
         col = rank & (cols - 1)
         start = jnp.sum(jnp.where(tile < my_tile, 1.0, 0.0), axis=1, keepdims=True).astype(i32)
         base = start + ((col - start) & (cols - 1))
-        turn_slot = right(rank - base + 16 * cols * obs, shift_of(cols)) - 16 * obs - turn * SLOTS
+        place = right(rank - base + cols * obs, shift_of(cols)) - obs
         local = rows - first
-        inside = (local >= 0) & (local < rows_dev) & (turn_slot >= 0) & (turn_slot < SLOTS)
-        slot = jnp.where(inside, col * per_col + b * SLOTS + turn_slot, -1)
+        inside = (local >= 0) & (local < rows_dev) & (place >= 0) & (place < SLOTS)
+        slot = jnp.where(inside, col * per_col + b * SLOTS + place, -1)
         pick += nt(one_hot(iota((slots, obs), 0) == slot),
                    one_hot(iota((rows_dev, obs), 0) == local))
     send_ref[...] = exact_nt(pick.astype(bf16), state_ref[...])
 
 
-def place_kernel(dims, where_ref, index_ref, slots_ref, held_ref, out_ref):
+def dense_kernel(dims, where_ref, index_ref, state_ref, send_ref):
+    tile_rows, _, cols, each_row = dims
+    _, rows_dev = state_ref.shape
+    batches, obs = index_ref.shape
+    width = 128
+    spots = []
+    for b in range(batches):
+        rows = index_ref[b:b + 1, :]
+        _, rank = order_of(rows, tile_rows, obs)
+        item = b * (obs // cols) + right(rank, shift_of(cols))
+        spot = right(item, shift_of(each_row)) * (cols * each_row)
+        spot = spot + (rank & (cols - 1)) * each_row + (item & (each_row - 1))
+        spots.append((spot, one_hot(iota((rows_dev, obs), 0) == rows - where_ref[1])))
+
+    def part(ds, at, carry):
+        pick = jnp.zeros((width, rows_dev), f32)
+        for spot, local in spots:
+            pick += nt(one_hot(iota((width, obs), 0) + at == spot), local)
+        send_ref[ds, :] = exact_nt(pick.astype(bf16), state_ref[...])
+        return carry
+
+    pieces(send_ref.shape[0], width, part)
+
+
+def place_kernel(dims, where_ref, index_ref, slots_ref, out_ref):
     tile_rows, cols, sizes = dims
     batches, _ = index_ref.shape
     slots = slots_ref.shape[0]
-    my_col, turn = where_ref[0], where_ref[1]
-    mine = [where_ref[2 + k] for k in range(3)]
+    my_col = where_ref[0]
+    mine = [where_ref[1 + k] for k in range(3)]
     half = out_ref.shape[0] // batches
     p = iota((slots, 1), 0)
     block = right(p, shift_of(batches * SLOTS))
     batch = right(p, shift_of(SLOTS)) & (batches - 1)
-    slot = (p & (SLOTS - 1)) + turn * SLOTS
+    slot = p & (SLOTS - 1)
     nx, nz, nc = sizes
     block_z = block & (nz - 1)
     block_x = right(block, shift_of(nz)) & (nx - 1)
@@ -153,7 +175,7 @@
     target = jnp.where((rank < end) & (j >= 0) & (j < half), batch * half + j, -1)
     wide = 128
     hot = jnp.where(iota((slots, wide), 1) == target, 1.0, 0.0).T.astype(bf16)
-    out_ref[...] = held_ref[...] + exact_nn(hot[0:out_ref.shape[0]], slots_ref[...])
+    out_ref[...] = exact_nn(hot[0:out_ref.shape[0]], slots_ref[...])
 
 
 def taper(first, second):
@@ -164,12 +186,17 @@
 def put_in_place(where, source_a, source_b, target, skip, stride, nzl, ny):
     zl, y, core = where
     unit = target.shape[0] // (2 * nzl * ny)
-    for source, half in ((source_a, core), (source_b, 1 - core)):
-        for dy in range(ny):
-            for dz in range(nzl):
-                at = ((((zl - dz) & (nzl - 1)) * ny + ((y - dy) & (ny - 1))) * 2 + half) * unit
-                k = ((dy * nzl + dz) * stride + skip) * unit
-                target[pl.ds(pl.multiple_of(at, unit), unit), :] = source[k:k + unit, :]
+
+    def step(k, carry):
+        dy, dz = right(k, shift_of(nzl)), k & (nzl - 1)
+        at = ((zl - dz) & (nzl - 1)) * ny + ((y - dy) & (ny - 1))
+        begin = pl.ds(pl.multiple_of((k * stride + skip) * unit, unit), unit)
+        for source, half in ((source_a, core), (source_b, 1 - core)):
+            to = pl.multiple_of((at * 2 + half) * unit, unit)
+            target[pl.ds(to, unit), :] = source[begin, :]
+        return carry
+
+    lax.fori_loop(0, nzl * ny, step, 0)
 
 
 def pieces(size, width, body, carry=0):
@@ -178,6 +205,14 @@
         return body(pl.ds(pl.multiple_of(at, width), width), at, carry)
 
     return lax.fori_loop(0, size // width, step, carry)
+
+
+def loop(size, width, body):
+    def step(ds, at, carry):
+        body(ds, at)
+        return carry
+
+    pieces(size, width, step)
 
 
 def each(size, width, body):
@@ -199,7 +234,7 @@
         part = part - jnp.mean(part, axis=1, keepdims=True)
         high[ds, :], middle[ds, :], low[ds, :] = split3(part)
 
-    each(o.shape[0], 128, rows)
+    loop(o.shape[0], 128, rows)
 
 
 def invert(pos_r, var_r, pos_c, members, high, middle, low, left, gram, other, spare, s_high, s_low,
@@ -229,7 +264,7 @@
         gram[:, ds] = scaled
         s_high[:, ds], s_low[:, ds] = split2(scaled)
 
-    each(obs, width, rescale)
+    loop(obs, 128, rescale)
 
     def squared(ds, at):
         square = nn(s_high[...], s_high[:, ds])
@@ -249,12 +284,12 @@
     factor, low_end = widen(alpha * lower)
 
     def first(ds, at):
-        ident = ident_part(obs, width, at)
+        ident = ident_part(obs, 128, at)
         step = alpha * gram[:, ds]
         xa[:, ds] = (factor * alpha * (2.0 * ident - step)).astype(bf16)
         ra[:, ds] = (ident - factor * (2.0 * step - alpha * alpha * left[:, ds])).astype(bf16)
 
-    each(obs, width, first)
+    loop(obs, 128, first)
 
     def grow(old, new, factor):
         def part(ds, at):
@@ -308,7 +343,7 @@
         def start(ds, at):
             left[:, ds] = ident_part(obs, narrow, at) * guess
 
-        each(obs, narrow, start)
+        loop(obs, narrow, start)
 
         def blocks(body, carry):
             def across(ds, at, carry):
@@ -345,7 +380,7 @@
         part = val_r + deviation * n[ds, :] - o[:, ds].T
         vh[ds, :], vl[ds, :] = split2(part * scale_r)
 
-    each(n.shape[0], 128, rows)
+    loop(n.shape[0], 128, rows)
 
 
 def weigh(pos_c, pos_dev, x, high, middle, members):
@@ -453,42 +488,54 @@
             compiler_params=pltpu.CompilerParams(vmem_limit_bytes=room << 20),
         )(*inputs)
 
+    send = call(
+        functools.partial(send_kernel, prep_dims),
+        jax.ShapeDtypeStruct((slots, members), f32),
+        (scalars(my_tile, first), obs_index, state), flops=1 << 28)
+    mine = lax.all_to_all(send.reshape(cols, batches * SLOTS, members), COL, 0, 0, tiled=True)
     par, noise_t = call(
         functools.partial(par_kernel, (bin_rows, tile_rows, cols)),
-        (jax.ShapeDtypeStruct((4 * batches, obs), f32), jax.ShapeDtypeStruct(noise.shape, f32)),
+        (jax.ShapeDtypeStruct((4 * batches, obs), f32),
+         jax.ShapeDtypeStruct(noise.shape, f32)),
         (scalars(0), obs_index, obs_values, obs_var, noise), flops=1 << 30)
-
-    def exchange(turn, held):
+    mine = jnp.sum(mine, axis=0)
+    mine = ring_gather(mine, "zh", nz)
+    mine = ring_gather(mine, "x", nx)
+    mine = ring_gather(mine, "core", nc)
+    held = call(
+        functools.partial(place_kernel, (tile_rows, cols, (nx, nz, nc))),
+        jax.ShapeDtypeStruct((batches * unit, members), f32),
+        (scalars(my_col, *(lax.axis_index(a) for a in ROW)), obs_index, mine),
+        flops=1 << 28)
+
+    def dense(held):
+        tiles_all = nx * nz * nc
+        each_row = batches * obs // cols // tiles_all
         send = call(
-            functools.partial(send_kernel, prep_dims),
-            jax.ShapeDtypeStruct((slots, members), f32),
-            (scalars(my_tile, first, turn), obs_index, state), flops=1 << 28)
-        mine = lax.all_to_all(send.reshape(cols, batches * SLOTS, members), COL, 0, 0, tiled=True)
+            functools.partial(dense_kernel, prep_dims + (each_row,)),
+            jax.ShapeDtypeStruct((batches * obs, members), f32),
+            (scalars(my_tile, first), obs_index, state))
+        mine = lax.all_to_all(
+            send.reshape(tiles_all * cols, each_row, members), ROW_COL, 0, 0, tiled=True)
         mine = jnp.sum(mine, axis=0)
-        mine = ring_gather(mine, "zh", nz)
-        mine = ring_gather(mine, "x", nx)
-        mine = ring_gather(mine, "core", nc)
-        return call(
-            functools.partial(place_kernel, (tile_rows, cols, (nx, nz, nc))),
-            jax.ShapeDtypeStruct((batches * unit, members), f32),
-            (scalars(my_col, turn, *(lax.axis_index(a) for a in ROW)), obs_index, mine, held),
-            flops=1 << 28)
+        copies = jnp.broadcast_to(mine, (tiles_all, *mine.shape))
+        mine = lax.all_to_all(copies, ROW, 0, 0, tiled=True)
+        mine = mine.reshape(batches, nc, unit, members)
+        return lax.dynamic_index_in_dim(mine, core, 1, keepdims=False).reshape(held.shape)
 
     tiles = obs_index[:, :, None] // tile_rows == jnp.arange(nx * nz * nc, dtype=i32)
-    most = jnp.max(jnp.sum(tiles.astype(i32), axis=1))
-    turns = (most + cols * SLOTS - 1) // (cols * SLOTS)
-    held = lax.fori_loop(0, turns, exchange, jnp.zeros((batches * unit, members), f32))
+    crowded = jnp.max(jnp.sum(tiles.astype(i32), axis=1)) > cols * SLOTS
+    held = lax.cond(crowded, dense, lambda held: held, held)
 
     swap = [(0, 1), (1, 0)]
     part = noise.shape[1] // nc
     noise_half = lax.dynamic_slice_in_dim(noise_t, core * part, part, axis=1)
     na = ring_gather(noise_half.reshape(batches * part, obs), "zl", nzl)
-    na, held = lax.optimization_barrier((na, held))
     na = ring_gather(na, "y", ny)
+    nb = lax.ppermute(na, "core", swap)
     oa = ring_gather(held, "zl", nzl)
     oa = ring_gather(oa, "y", ny)
     ob = lax.ppermute(oa, "core", swap)
-    nb = lax.ppermute(na, "core", swap)
     full = (obs, members)
     wide, slim = pltpu.VMEM(full, f32), pltpu.VMEM(full, bf16)
     where = scalars(lax.axis_index("zl"), lax.axis_index("y"), core, first)

time: 390 us -> 389 us (level)
  blocking collectives: 16.4 us -> 0 us
  starting transfers between devices: 28.3 us -> 41.2 us
  Pallas kernels: 309 us -> 315 us
    all_to_all x1 -> x0, blocking collectives: 16.4 us -> none  [exchange(): lax.all_to_all(send.reshape(cols, batches * SLOTS, members), COL, 0, 0, t...]
    ppermute x17, starting transfers between devices: 28.1 us -> 34.6 us  [ring_gather(): lax.ppermute(value, axis, [(i, (i + k) % size) for i in range(size)])]
    all_to_all x0 -> x1, starting transfers between devices: none -> 5.95 us  [on_device(): lax.all_to_all(send.reshape(cols, batches * SLOTS, members), COL, 0, 0, t...]
    pallas_call x4, Pallas kernels: 309 us -> 315 us  [call(): pl.pallas_call(kernel, out_shape=shapes, in_specs=[smem] + [vmem] * (len(...]
  transfers between devices with their start and end apart: 19 -> 20, of which waited for: 12 -> 11; matrix products, arithmetic and copies ran while one was open for 0% -> 0% of each run, Pallas kernels for 0% -> 1%
where the time goes in v2:
time: 389 us; the launch traced here: 387 us
  Pallas kernels  315 us (81%)
  starting transfers between devices  41.2 us (11%)
  waiting for transfers between devices  26.9 us (7%)
    pallas_call x4, Pallas kernels, call(): pl.pallas_call(kernel, out_shape=shapes, in_specs=[smem] + [vmem] * (len(...  315 us
    ppermute x17, starting transfers between devices, ring_gather(): lax.ppermute(value, axis, [(i, (i + k) % size) for i in range(size)])  34.6 us
    ppermute x17, waiting for transfers between devices, ring_gather(): lax.ppermute(value, axis, [(i, (i + k) % size) for i in range(size)])  24.3 us
  transfers between devices with their start and end apart: 20, of which 11 were waited for; matrix products, arithmetic and copies ran while one was open for 0% of the time, Pallas kernels for 1%

profile of v2, /device:TPU:32, one launch (start us, length us, event | category | flops | bytes accessed | tf_op | source)
XLA Modules:
  0.0 387.5 jit_solution(14166336123635563166)
XLA Ops:
  0.0 0.9 copy-done
  2.3 1.7 shard_map.55
  4.0 2.0 collective-permute-start.12
  6.0 2.3 collective-permute-start.13
  8.3 1.1 collective-permute-start.14
  9.5 2.4 shard_map.56
  11.9 5.9 %all-to-all-start.2 = ((f32[16,8,512]{2,1,0:T(8,128)}), f32[16,8,512]{2,1,0:T(8,128)S(1)}, u32[]{:S(2)}, u32[]{:S(2)}) async-start(f32[16,8,512]{2,1,0:T(8,128)} %bitcast.12), calls=%async_computation.2 | async-start | bytes 524288 | tf_op jit(solution)/shard_map/all_to_all | solution.py:495
  19.5 1.5 collective-permute-start.15
  21.1 2.7 collective-permute-start.16
  23.7 1.5 collective-permute-start.17
  25.2 5.2 %collective-permute-done.15 = f32[128,512]{1,0:T(8,128)S(1)} collective-permute-done((f32[128,512]{1,0:T(8,128)S(1)}, f32[128,512]{1,0:T(8,128)S(1)}, u32[]{:S(2)}, u32[]{:S(2)}) %collective-permute-start.15) | collective-permute-done | bytes 262176 | tf_op jit(solution)/shard_map/ppermute | solution.py:451
  30.6 5.9 %collective-permute-start = (f32[8,512]{1,0:T(8,128)S(1)}, f32[8,512]{1,0:T(8,128)S(1)}, u32[]{:S(2)}, u32[]{:S(2)}) collective-permute-start(f32[8,512]{1,0:T(8,128)S(1)} %reduce_sum.28), channel_id=1, source_target_pairs={{0,32},{32,0},{1,33},{33,1},{2,34},{34,2},{3,35},{35,3},{4,36},{36... | collective-permute-start | bytes 49160 | tf_op jit(solution)/shard_map/ppermute | solution.py:451
  36.5 1.8 collective-permute-done
  38.3 1.5 collective-permute-start.1
  39.8 2.7 collective-permute-start.2
  42.5 1.4 collective-permute-start.3
  44.0 1.2 collective-permute-done.2
  45.2 1.2 collective-permute-done.3
  47.8 0.9 shard_map.57
  48.9 1.5 collective-permute-start.5
  50.4 1.0 collective-permute-start.6
  51.4 1.2 collective-permute-start.7
  52.6 2.3 collective-permute-done.5
  54.9 1.0 collective-permute-done.6
  55.9 1.9 collective-permute-done.7
  57.8 0.7 collective-permute-start.8
  58.5 5.0 %collective-permute-start.9 = (f32[128,512]{1,0:T(8,128)S(1)}, f32[128,512]{1,0:T(8,128)S(1)}, u32[]{:S(2)}, u32[]{:S(2)}) collective-permute-start(f32[128,512]{1,0:T(8,128)S(1)} %pad_maximum_fusion), channel_id=1, source_target_pairs={{0,2},{1,3},{2,0},{3,1},{4,6},{5,7},{6,4},{7,5},{8,10},{9,11},{10,... | collective-permute-start | bytes 786440 | tf_op jit(solution)/shard_map/ppermute | solution.py:451
  63.6 2.5 collective-permute-start.10
  66.1 1.1 collective-permute-done.8
  67.2 7.8 %collective-permute-done.9 = f32[128,512]{1,0:T(8,128)S(1)} collective-permute-done((f32[128,512]{1,0:T(8,128)S(1)}, f32[128,512]{1,0:T(8,128)S(1)}, u32[]{:S(2)}, u32[]{:S(2)}) %collective-permute-start.9) | collective-permute-done | bytes 262176 | tf_op jit(solution)/shard_map/ppermute | solution.py:451
  75.3 2.6 collective-permute-done.11.ob
  77.9 309.6 %shard_map.58 = f32[512,256]{1,0:T(8,128)} custom-call(s32[4]{0:T(128)S(1)} %pad_add_fusion.1.where_ref, f32[8,512]{1,0:T(8,128)S(1)} %get-tuple-element.26.par_ref, f32[512,512]{1,0:T(8,128)S(1)} %constant_dynamic-update-slice_fusion.11.oa, f32[512,512]{1,0:T(8,128)S(1)} %collective-permute-done.11.ob, ...), custom_call_target="tpu_custom_call" | custom-call | flops 21474836480 | bytes 4194304 | tf_op jit(solution)/shard_map/pallas_call | solution.py:481
  (56 shorter events, 4.2 us)
Async XLA Ops:
  0.0 9.5 %copy-start.5 = (s32[2,512]{1,0:T(2,128)S(1)}, s32[2,512]{1,0:T(2,128)}, u32[]{:S(2)}) copy-start(s32[2,512]{1,0:T(2,128)} %index_ref.5) | copy-start | bytes 12292
  0.0 0.9 copy-start
  0.9 0.7 copy-start.1
  1.6 0.7 copy-start.2
  2.3 7.2 %copy-start.3 = (f32[512,256]{1,0:T(8,128)S(1)}, f32[512,256]{1,0:T(8,128)}, u32[]{:S(2)}) copy-start(f32[512,256]{1,0:T(8,128)} %x_ref.1) | copy-start | bytes 1572868
  4.0 15.5 %collective-permute-start.12 = (f32[32,512]{1,0:T(8,128)S(1)}, f32[32,512]{1,0:T(8,128)S(1)}, u32[]{:S(2)}, u32[]{:S(2)}) collective-permute-start(f32[32,512]{1,0:T(8,128)S(1)} %bitcast.15), channel_id=1, source_target_pairs={{0,4},{4,8},{8,12},{12,0},{1,5},{5,9},{9,13},{13,1},{2,6},{6,10},{... | collective-permute-start | bytes 196616 | tf_op jit(solution)/shard_map/ppermute | solution.py:451
  6.0 13.5 %collective-permute-start.13 = (f32[32,512]{1,0:T(8,128)S(1)}, f32[32,512]{1,0:T(8,128)S(1)}, u32[]{:S(2)}, u32[]{:S(2)}) collective-permute-start(f32[32,512]{1,0:T(8,128)S(1)} %bitcast.16), channel_id=1, source_target_pairs={{0,8},{4,12},{8,0},{12,4},{1,9},{5,13},{9,1},{13,5},{2,10},{6,14},... | collective-permute-start | bytes 196616 | tf_op jit(solution)/shard_map/ppermute | solution.py:451
  8.3 11.2 %collective-permute-start.14 = (f32[32,512]{1,0:T(8,128)S(1)}, f32[32,512]{1,0:T(8,128)S(1)}, u32[]{:S(2)}, u32[]{:S(2)}) collective-permute-start(f32[32,512]{1,0:T(8,128)S(1)} %bitcast.17), channel_id=1, source_target_pairs={{0,12},{4,0},{8,4},{12,8},{1,13},{5,1},{9,5},{13,9},{2,14},{6,2},{... | collective-permute-start | bytes 196616 | tf_op jit(solution)/shard_map/ppermute | solution.py:451
  11.9 18.6 %all-to-all-start.2 = ((f32[16,8,512]{2,1,0:T(8,128)}), f32[16,8,512]{2,1,0:T(8,128)S(1)}, u32[]{:S(2)}, u32[]{:S(2)}) async-start(f32[16,8,512]{2,1,0:T(8,128)} %bitcast.12), calls=%async_computation.2 | async-start | bytes 524288 | tf_op jit(solution)/shard_map/all_to_all | solution.py:495
  19.5 11.0 %collective-permute-start.15 = (f32[128,512]{1,0:T(8,128)S(1)}, f32[128,512]{1,0:T(8,128)S(1)}, u32[]{:S(2)}, u32[]{:S(2)}) collective-permute-start(f32[128,512]{1,0:T(8,128)S(1)} %pad_maximum_fusion.1), channel_id=1, source_target_pairs={{0,1},{1,2},{2,3},{3,0},{4,5},{5,6},{6,7},{7,4},{8,9},{9,10},{10,1... | collective-permute-start | bytes 786440 | tf_op jit(solution)/shard_map/ppermute | solution.py:451
  21.1 25.4 %collective-permute-start.16 = (f32[128,512]{1,0:T(8,128)S(1)}, f32[128,512]{1,0:T(8,128)S(1)}, u32[]{:S(2)}, u32[]{:S(2)}) collective-permute-start(f32[128,512]{1,0:T(8,128)S(1)} %pad_maximum_fusion.1), channel_id=1, source_target_pairs={{0,2},{1,3},{2,0},{3,1},{4,6},{5,7},{6,4},{7,5},{8,10},{9,11},{10,... | collective-permute-start | bytes 786440 | tf_op jit(solution)/shard_map/ppermute | solution.py:451
  23.7 22.7 %collective-permute-start.17 = (f32[128,512]{1,0:T(8,128)S(1)}, f32[128,512]{1,0:T(8,128)S(1)}, u32[]{:S(2)}, u32[]{:S(2)}) collective-permute-start(f32[128,512]{1,0:T(8,128)S(1)} %pad_maximum_fusion.1), channel_id=1, source_target_pairs={{0,3},{1,0},{2,1},{3,2},{4,7},{5,4},{6,5},{7,6},{8,11},{9,8},{10,9... | collective-permute-start | bytes 786440 | tf_op jit(solution)/shard_map/ppermute | solution.py:451
  30.6 7.7 %collective-permute-start = (f32[8,512]{1,0:T(8,128)S(1)}, f32[8,512]{1,0:T(8,128)S(1)}, u32[]{:S(2)}, u32[]{:S(2)}) collective-permute-start(f32[8,512]{1,0:T(8,128)S(1)} %reduce_sum.28), channel_id=1, source_target_pairs={{0,32},{32,0},{1,33},{33,1},{2,34},{34,2},{3,35},{35,3},{4,36},{36... | collective-permute-start | bytes 49160 | tf_op jit(solution)/shard_map/ppermute | solution.py:451
  38.3 5.7 %collective-permute-start.1 = (f32[16,512]{1,0:T(8,128)S(1)}, f32[16,512]{1,0:T(8,128)S(1)}, u32[]{:S(2)}, u32[]{:S(2)}) collective-permute-start(f32[16,512]{1,0:T(8,128)S(1)} %pad_maximum_fusion.2), channel_id=1, source_target_pairs={{0,64},{64,128},{128,192},{192,0},{1,65},{65,129},{129,193},{193,1... | collective-permute-start | bytes 98312 | tf_op jit(solution)/shard_map/ppermute | solution.py:451
  39.8 5.4 %collective-permute-start.2 = (f32[16,512]{1,0:T(8,128)S(1)}, f32[16,512]{1,0:T(8,128)S(1)}, u32[]{:S(2)}, u32[]{:S(2)}) collective-permute-start(f32[16,512]{1,0:T(8,128)S(1)} %pad_maximum_fusion.2), channel_id=1, source_target_pairs={{0,128},{64,192},{128,0},{192,64},{1,129},{65,193},{129,1},{193,65... | collective-permute-start | bytes 98312 | tf_op jit(solution)/shard_map/ppermute | solution.py:451
  42.5 3.9 %collective-permute-start.3 = (f32[16,512]{1,0:T(8,128)S(1)}, f32[16,512]{1,0:T(8,128)S(1)}, u32[]{:S(2)}, u32[]{:S(2)}) collective-permute-start(f32[16,512]{1,0:T(8,128)S(1)} %pad_maximum_fusion.2), channel_id=1, source_target_pairs={{0,192},{64,0},{128,64},{192,128},{1,193},{65,1},{129,65},{193,129... | collective-permute-start | bytes 98312 | tf_op jit(solution)/shard_map/ppermute | solution.py:451
  46.4 1.3 collective-permute-start.4
  46.5 28.8 %collective-permute-start.18 = (f32[512,512]{1,0:T(8,128)S(1)}, f32[512,512]{1,0:T(8,128)}, u32[]{:S(2)}, u32[]{:S(2)}) collective-permute-start(f32[512,512]{1,0:T(8,128)S(1)} %constant_dynamic-update-slice_fusion.18.na), channel_id=1, source_target_pairs={{0,16},{16,0},{1,17},{17,1},{2,18},{18,2},{3,19},{19,3},{4,20},{20... | collective-permute-start | bytes 3145736 | tf_op jit(solution)/shard_map/ppermute | solution.py:535
  48.8 29.0 %copy-start.4 = (f32[512,256]{1,0:T(8,128)S(1)}, f32[512,256]{1,0:T(8,128)}, u32[]{:S(2)}) copy-start(f32[512,256]{1,0:T(8,128)} %x_ref.1) | copy-start | bytes 1572868
  48.9 6.0 %collective-permute-start.5 = (f32[32,512]{1,0:T(8,128)S(1)}, f32[32,512]{1,0:T(8,128)S(1)}, u32[]{:S(2)}, u32[]{:S(2)}) collective-permute-start(f32[32,512]{1,0:T(8,128)S(1)} %get-tuple-element.38), channel_id=1, source_target_pairs={{0,4},{4,8},{8,12},{12,0},{1,5},{5,9},{9,13},{13,1},{2,6},{6,10},{... | collective-permute-start | bytes 196616 | tf_op jit(solution)/shard_map/ppermute | solution.py:451
  50.4 5.5 %collective-permute-start.6 = (f32[32,512]{1,0:T(8,128)S(1)}, f32[32,512]{1,0:T(8,128)S(1)}, u32[]{:S(2)}, u32[]{:S(2)}) collective-permute-start(f32[32,512]{1,0:T(8,128)S(1)} %get-tuple-element.38), channel_id=1, source_target_pairs={{0,8},{4,12},{8,0},{12,4},{1,9},{5,13},{9,1},{13,5},{2,10},{6,14},... | collective-permute-start | bytes 196616 | tf_op jit(solution)/shard_map/ppermute | solution.py:451
  51.4 6.4 %collective-permute-start.7 = (f32[32,512]{1,0:T(8,128)S(1)}, f32[32,512]{1,0:T(8,128)S(1)}, u32[]{:S(2)}, u32[]{:S(2)}) collective-permute-start(f32[32,512]{1,0:T(8,128)S(1)} %get-tuple-element.38), channel_id=1, source_target_pairs={{0,12},{4,0},{8,4},{12,8},{1,13},{5,1},{9,5},{13,9},{2,14},{6,2},{... | collective-permute-start | bytes 196616 | tf_op jit(solution)/shard_map/ppermute | solution.py:451
  57.8 9.4 %collective-permute-start.8 = (f32[128,512]{1,0:T(8,128)S(1)}, f32[128,512]{1,0:T(8,128)S(1)}, u32[]{:S(2)}, u32[]{:S(2)}) collective-permute-start(f32[128,512]{1,0:T(8,128)S(1)} %pad_maximum_fusion), channel_id=1, source_target_pairs={{0,1},{1,2},{2,3},{3,0},{4,5},{5,6},{6,7},{7,4},{8,9},{9,10},{10,1... | collective-permute-start | bytes 786440 | tf_op jit(solution)/shard_map/ppermute | solution.py:451
  58.5 16.5 %collective-permute-start.9 = (f32[128,512]{1,0:T(8,128)S(1)}, f32[128,512]{1,0:T(8,128)S(1)}, u32[]{:S(2)}, u32[]{:S(2)}) collective-permute-start(f32[128,512]{1,0:T(8,128)S(1)} %pad_maximum_fusion), channel_id=1, source_target_pairs={{0,2},{1,3},{2,0},{3,1},{4,6},{5,7},{6,4},{7,5},{8,10},{9,11},{10,... | collective-permute-start | bytes 786440 | tf_op jit(solution)/shard_map/ppermute | solution.py:451
  63.6 11.5 %collective-permute-start.10 = (f32[128,512]{1,0:T(8,128)S(1)}, f32[128,512]{1,0:T(8,128)S(1)}, u32[]{:S(2)}, u32[]{:S(2)}) collective-permute-start(f32[128,512]{1,0:T(8,128)S(1)} %pad_maximum_fusion), channel_id=1, source_target_pairs={{0,3},{1,0},{2,1},{3,2},{4,7},{5,4},{6,5},{7,6},{8,11},{9,8},{10,9... | collective-permute-start | bytes 786440 | tf_op jit(solution)/shard_map/ppermute | solution.py:451
  75.1 2.7 collective-permute-start.11

commit v3 on v2

--- a/solution.py
+++ b/solution.py
@@ -187,16 +187,13 @@
     zl, y, core = where
     unit = target.shape[0] // (2 * nzl * ny)
 
-    def step(k, carry):
-        dy, dz = right(k, shift_of(nzl)), k & (nzl - 1)
+    for k in range(nzl * ny):
+        dy, dz = divmod(k, nzl)
         at = ((zl - dz) & (nzl - 1)) * ny + ((y - dy) & (ny - 1))
-        begin = pl.ds(pl.multiple_of((k * stride + skip) * unit, unit), unit)
+        begin = (k * stride + skip) * unit
         for source, half in ((source_a, core), (source_b, 1 - core)):
             to = pl.multiple_of((at * 2 + half) * unit, unit)
-            target[pl.ds(to, unit), :] = source[begin, :]
-        return carry
-
-    lax.fori_loop(0, nzl * ny, step, 0)
+            target[pl.ds(to, unit), :] = source[begin:begin + unit, :]
 
 
 def pieces(size, width, body, carry=0):
@@ -228,29 +225,28 @@
     return jnp.where(eye_part(obs, width, at), 1.0, 0.0)
 
 
-def centre(o, high, middle, low):
+def centre(o, high, middle):
     def rows(ds, at):
         part = o[ds, :]
         part = part - jnp.mean(part, axis=1, keepdims=True)
-        high[ds, :], middle[ds, :], low[ds, :] = split3(part)
-
-    loop(o.shape[0], 128, rows)
-
-
-def invert(pos_r, var_r, pos_c, members, high, middle, low, left, gram, other, spare, s_high, s_low,
-           xa, xb, ra, rb, eh, el, vec):
+        high[ds, :], middle[ds, :] = split2(part)
+
+    each(o.shape[0], 128, rows)
+
+
+def invert(pos_r, var_r, pos_c, members, high, middle, left, gram, other, spare, s_high, s_low,
+           xa, xb, ra, rb, eh, vec):
     obs = gram.shape[0]
     width = obs
     norming = 1.0 / (members - 1)
 
     def cross_terms(ds, at):
-        left[:, ds] = nt(high[...], middle[ds, :]) + nt(high[...], low[ds, :])
+        left[:, ds] = nt(high[...], middle[ds, :])
 
     each(obs, width, cross_terms)
 
     def covariance(ds, at):
-        product = nt(high[...], high[ds, :]) + nt(middle[...], middle[ds, :])
-        product = product + left[:, ds] + left[ds, :].T
+        product = nt(high[...], high[ds, :]) + left[:, ds] + left[ds, :].T
         eye = eye_part(obs, width, at)
         covar = taper(pos_c, pos_r[:, ds]) * product * norming + jnp.where(eye, var_r[:, ds], 0.0)
         gram[:, ds] = covar
@@ -264,7 +260,7 @@
         gram[:, ds] = scaled
         s_high[:, ds], s_low[:, ds] = split2(scaled)
 
-    loop(obs, 128, rescale)
+    each(obs, 128, rescale)
 
     def squared(ds, at):
         square = nn(s_high[...], s_high[:, ds])
@@ -289,7 +285,7 @@
         xa[:, ds] = (factor * alpha * (2.0 * ident - step)).astype(bf16)
         ra[:, ds] = (ident - factor * (2.0 * step - alpha * alpha * left[:, ds])).astype(bf16)
 
-    loop(obs, 128, first)
+    each(obs, 128, first)
 
     def grow(old, new, factor):
         def part(ds, at):
@@ -327,7 +323,7 @@
     each(obs, width, second_order)
 
     def correction(ds, at):
-        eh[:, ds], el[:, ds] = split2(nn(xb[...], rb[:, ds]))
+        eh[:, ds] = nn(xb[...], rb[:, ds]).astype(bf16)
 
     each(obs, width, correction)
     size = jnp.max(vec[1:2, :], axis=1, keepdims=True)
@@ -370,7 +366,7 @@
         lax.while_loop(lambda c: (c[0] < 40) & jnp.logical_not(c[1] < 1e-7), advance,
                        (jnp.int32(0), jnp.float32(1.0)))
         xb[...] = left[...].astype(bf16)
-        eh[...], el[...] = split2(left[...] - xb[...].astype(f32))
+        eh[...] = (left[...] - xb[...].astype(f32)).astype(bf16)
 
 
 def innovate(val_r, var_r, scale_r, o, n, vh, vl):
@@ -380,7 +376,7 @@
         part = val_r + deviation * n[ds, :] - o[:, ds].T
         vh[ds, :], vl[ds, :] = split2(part * scale_r)
 
-    loop(n.shape[0], 128, rows)
+    each(n.shape[0], 128, rows)
 
 
 def weigh(pos_c, pos_dev, x, high, middle, members):
@@ -398,30 +394,29 @@
 
 
 def main_kernel(dims, where_ref, par_ref, oa, ob, na, nb, x_ref, out_ref,
-                high0, middle0, high, middle, o0, o, n, vh, vl, sh, sl, xb, eh, el, vec, *work):
+                high0, middle0, high, middle, o0, o, n, vh, vl, sh, sl, xb, eh, vec, *work):
     bin_rows, nzl, ny = dims
     where = [where_ref[k] for k in range(3)]
     obs, members = o.shape
-    low, left, gram, other, spare, s_high, s_low, xa, ra, rb = work
+    left, gram, other, spare, s_high, s_low, xa, ra, rb = work
     cols_par = columns(par_ref)
     pos_dev = own_positions(where_ref[3], x_ref.shape[1], bin_rows)
     norming = 1.0 / (members - 1)
     put_in_place(where, oa, ob, o0, 0, 2, nzl, ny)
     put_in_place(where, na, nb, n, 0, 2, nzl, ny)
     pos_c = cols_par[:, 0:1]
-    centre(o0, high0, middle0, low)
-    invert(par_ref.at[0:1], par_ref.at[2:3], pos_c, members, high0, middle0, low, left, gram,
-           other, spare, s_high, s_low, xa, xb, ra, rb, eh, el, vec)
+    centre(o0, high0, middle0)
+    invert(par_ref.at[0:1], par_ref.at[2:3], pos_c, members, high0, middle0, left, gram,
+           other, spare, s_high, s_low, xa, xb, ra, rb, eh, vec)
     innovate(par_ref[1:2, :], par_ref[2:3, :], vec[0:1, :], o0, n, vh, vl)
     solved = nn(vh[...], xb[...]) + nn(vl[...], xb[...]) + nn(vh[...], eh[...])
-    solved = solved + nn(vh[...], el[...])
     sh[...], sl[...] = split2(solved * vec[0:1, :])
     wh, wl = split2(weigh(pos_c, pos_dev, x_ref[...], high0, middle0, members))
     out_ref[...] = x_ref[...] + nn(sh[...], wh) + nn(sh[...], wl) + nn(sl[...], wh)
     put_in_place(where, oa, ob, o, 1, 2, nzl, ny)
     put_in_place(where, na, nb, n, 1, 2, nzl, ny)
     pos_c = cols_par[:, 4:5]
-    centre(o, high, middle, low)
+    centre(o, high, middle)
 
     def weights(ds, at):
         cross = nt(high[...], high0[ds, :]) + nt(high[...], middle0[ds, :])
@@ -435,12 +430,12 @@
                     + nt(xb[...], sh[ds, :]))
 
     each(members, members, update)
-    centre(o, high, middle, low)
-    invert(par_ref.at[4:5], par_ref.at[6:7], pos_c, members, high, middle, low, left, gram, other,
-           spare, s_high, s_low, xa, xb, ra, rb, eh, el, vec)
+    centre(o, high, middle)
+    invert(par_ref.at[4:5], par_ref.at[6:7], pos_c, members, high, middle, left, gram, other,
+           spare, s_high, s_low, xa, xb, ra, rb, eh, vec)
     scale_c = column_of(vec[0:1, :])
     wh, wl = split2(weigh(pos_c, pos_dev, out_ref[...], high, middle, members) * scale_c)
-    applied = nn(xb[...], wh) + nn(xb[...], wl) + nn(eh[...], wh) + nn(el[...], wh)
+    applied = nn(xb[...], wh) + nn(xb[...], wl) + nn(eh[...], wh)
     wh, wl = split2(applied * scale_c)
     innovate(par_ref[5:6, :], par_ref[6:7, :], jnp.ones((1, obs), f32), o, n, vh, vl)
     out_ref[...] = out_ref[...] + nn(vh[...], wh) + nn(vh[...], wl) + nn(vl[...], wh)
@@ -543,8 +538,8 @@
         functools.partial(main_kernel, (bin_rows, nzl, ny)),
         jax.ShapeDtypeStruct(state.shape, f32),
         (where, par, oa, ob, na, nb, state),
-        scratch=([slim] * 4 + [wide] * 3 + [slim] * 7 + [pltpu.VMEM((8, obs), f32)]
-                 + [slim] + [wide] * 4 + [slim] * 5),
+        scratch=([slim] * 4 + [wide] * 3 + [slim] * 6 + [pltpu.VMEM((8, obs), f32)]
+                 + [wide] * 4 + [slim] * 5),
         flops=20 << 30, room=32)
 
 

time: 389 us -> 382 us (0.982)
  Pallas kernels: 315 us -> 308 us
    pallas_call x4, Pallas kernels: 315 us -> 308 us  [call(): pl.pallas_call(kernel, out_shape=shapes, in_specs=[smem] + [vmem] * (len(...]
where the time goes in v3:
time: 382 us; the launch traced here: 381 us
  Pallas kernels  308 us (81%)
  starting transfers between devices  41.2 us (11%)
  waiting for transfers between devices  26.9 us (7%)
    pallas_call x4, Pallas kernels, call(): pl.pallas_call(kernel, out_shape=shapes, in_specs=[smem] + [vmem] * (len(...  308 us
    ppermute x17, starting transfers between devices, ring_gather(): lax.ppermute(value, axis, [(i, (i + k) % size) for i in range(size)])  34.6 us
    ppermute x17, waiting for transfers between devices, ring_gather(): lax.ppermute(value, axis, [(i, (i + k) % size) for i in range(size)])  24.3 us
  transfers between devices with their start and end apart: 20, of which 11 were waited for; matrix products, arithmetic and copies ran while one was open for 0% of the time, Pallas kernels for 1%

profile of v3, /device:TPU:32, one launch (start us, length us, event | category | flops | bytes accessed | tf_op | source)
XLA Modules:
  0.0 381.3 jit_solution(16851249101327610483)
XLA Ops:
  0.0 0.9 copy-done
  2.3 1.7 shard_map.55
  4.0 2.0 collective-permute-start.12
  6.0 2.3 collective-permute-start.13
  8.3 1.1 collective-permute-start.14
  9.5 2.4 shard_map.56
  11.9 5.9 %all-to-all-start.2 = ((f32[16,8,512]{2,1,0:T(8,128)}), f32[16,8,512]{2,1,0:T(8,128)S(1)}, u32[]{:S(2)}, u32[]{:S(2)}) async-start(f32[16,8,512]{2,1,0:T(8,128)} %bitcast.12), calls=%async_computation.2 | async-start | bytes 524288 | tf_op jit(solution)/shard_map/all_to_all | solution.py:490
  19.5 1.5 collective-permute-start.15
  21.1 2.7 collective-permute-start.16
  23.7 1.5 collective-permute-start.17
  25.2 5.2 %collective-permute-done.15 = f32[128,512]{1,0:T(8,128)S(1)} collective-permute-done((f32[128,512]{1,0:T(8,128)S(1)}, f32[128,512]{1,0:T(8,128)S(1)}, u32[]{:S(2)}, u32[]{:S(2)}) %collective-permute-start.15) | collective-permute-done | bytes 262176 | tf_op jit(solution)/shard_map/ppermute | solution.py:446
  30.6 5.9 %collective-permute-start = (f32[8,512]{1,0:T(8,128)S(1)}, f32[8,512]{1,0:T(8,128)S(1)}, u32[]{:S(2)}, u32[]{:S(2)}) collective-permute-start(f32[8,512]{1,0:T(8,128)S(1)} %reduce_sum.28), channel_id=1, source_target_pairs={{0,32},{32,0},{1,33},{33,1},{2,34},{34,2},{3,35},{35,3},{4,36},{36... | collective-permute-start | bytes 49160 | tf_op jit(solution)/shard_map/ppermute | solution.py:446
  36.5 1.8 collective-permute-done
  38.3 1.5 collective-permute-start.1
  39.8 2.7 collective-permute-start.2
  42.5 1.4 collective-permute-start.3
  44.0 1.2 collective-permute-done.2
  45.2 1.2 collective-permute-done.3
  47.8 0.9 shard_map.57
  48.9 1.5 collective-permute-start.5
  50.4 1.0 collective-permute-start.6
  51.4 1.2 collective-permute-start.7
  52.6 2.3 collective-permute-done.5
  54.9 1.0 collective-permute-done.6
  55.9 1.9 collective-permute-done.7
  57.8 0.7 collective-permute-start.8
  58.5 5.0 %collective-permute-start.9 = (f32[128,512]{1,0:T(8,128)S(1)}, f32[128,512]{1,0:T(8,128)S(1)}, u32[]{:S(2)}, u32[]{:S(2)}) collective-permute-start(f32[128,512]{1,0:T(8,128)S(1)} %pad_maximum_fusion), channel_id=1, source_target_pairs={{0,2},{1,3},{2,0},{3,1},{4,6},{5,7},{6,4},{7,5},{8,10},{9,11},{10,... | collective-permute-start | bytes 786440 | tf_op jit(solution)/shard_map/ppermute | solution.py:446
  63.6 2.5 collective-permute-start.10
  66.1 1.1 collective-permute-done.8
  67.2 7.8 %collective-permute-done.9 = f32[128,512]{1,0:T(8,128)S(1)} collective-permute-done((f32[128,512]{1,0:T(8,128)S(1)}, f32[128,512]{1,0:T(8,128)S(1)}, u32[]{:S(2)}, u32[]{:S(2)}) %collective-permute-start.9) | collective-permute-done | bytes 262176 | tf_op jit(solution)/shard_map/ppermute | solution.py:446
  75.3 2.6 collective-permute-done.11.ob
  77.9 303.4 %shard_map.58 = f32[512,256]{1,0:T(8,128)} custom-call(s32[4]{0:T(128)S(1)} %pad_add_fusion.1.where_ref, f32[8,512]{1,0:T(8,128)S(1)} %get-tuple-element.26.par_ref, f32[512,512]{1,0:T(8,128)S(1)} %constant_dynamic-update-slice_fusion.11.oa, f32[512,512]{1,0:T(8,128)S(1)} %collective-permute-done.11.ob, ...), custom_call_target="tpu_custom_call" | custom-call | flops 21474836480 | bytes 4194304 | tf_op jit(solution)/shard_map/pallas_call | solution.py:476
  (56 shorter events, 4.2 us)
Async XLA Ops:
  0.0 9.5 %copy-start.5 = (s32[2,512]{1,0:T(2,128)S(1)}, s32[2,512]{1,0:T(2,128)}, u32[]{:S(2)}) copy-start(s32[2,512]{1,0:T(2,128)} %index_ref.5) | copy-start | bytes 12292
  0.0 0.9 copy-start
  0.9 0.7 copy-start.1
  1.6 0.7 copy-start.2
  2.3 7.2 %copy-start.3 = (f32[512,256]{1,0:T(8,128)S(1)}, f32[512,256]{1,0:T(8,128)}, u32[]{:S(2)}) copy-start(f32[512,256]{1,0:T(8,128)} %x_ref.1) | copy-start | bytes 1572868
  4.0 15.5 %collective-permute-start.12 = (f32[32,512]{1,0:T(8,128)S(1)}, f32[32,512]{1,0:T(8,128)S(1)}, u32[]{:S(2)}, u32[]{:S(2)}) collective-permute-start(f32[32,512]{1,0:T(8,128)S(1)} %bitcast.15), channel_id=1, source_target_pairs={{0,4},{4,8},{8,12},{12,0},{1,5},{5,9},{9,13},{13,1},{2,6},{6,10},{... | collective-permute-start | bytes 196616 | tf_op jit(solution)/shard_map/ppermute | solution.py:446
  6.0 13.5 %collective-permute-start.13 = (f32[32,512]{1,0:T(8,128)S(1)}, f32[32,512]{1,0:T(8,128)S(1)}, u32[]{:S(2)}, u32[]{:S(2)}) collective-permute-start(f32[32,512]{1,0:T(8,128)S(1)} %bitcast.16), channel_id=1, source_target_pairs={{0,8},{4,12},{8,0},{12,4},{1,9},{5,13},{9,1},{13,5},{2,10},{6,14},... | collective-permute-start | bytes 196616 | tf_op jit(solution)/shard_map/ppermute | solution.py:446
  8.3 11.2 %collective-permute-start.14 = (f32[32,512]{1,0:T(8,128)S(1)}, f32[32,512]{1,0:T(8,128)S(1)}, u32[]{:S(2)}, u32[]{:S(2)}) collective-permute-start(f32[32,512]{1,0:T(8,128)S(1)} %bitcast.17), channel_id=1, source_target_pairs={{0,12},{4,0},{8,4},{12,8},{1,13},{5,1},{9,5},{13,9},{2,14},{6,2},{... | collective-permute-start | bytes 196616 | tf_op jit(solution)/shard_map/ppermute | solution.py:446
  11.9 18.6 %all-to-all-start.2 = ((f32[16,8,512]{2,1,0:T(8,128)}), f32[16,8,512]{2,1,0:T(8,128)S(1)}, u32[]{:S(2)}, u32[]{:S(2)}) async-start(f32[16,8,512]{2,1,0:T(8,128)} %bitcast.12), calls=%async_computation.2 | async-start | bytes 524288 | tf_op jit(solution)/shard_map/all_to_all | solution.py:490
  19.5 11.0 %collective-permute-start.15 = (f32[128,512]{1,0:T(8,128)S(1)}, f32[128,512]{1,0:T(8,128)S(1)}, u32[]{:S(2)}, u32[]{:S(2)}) collective-permute-start(f32[128,512]{1,0:T(8,128)S(1)} %pad_maximum_fusion.1), channel_id=1, source_target_pairs={{0,1},{1,2},{2,3},{3,0},{4,5},{5,6},{6,7},{7,4},{8,9},{9,10},{10,1... | collective-permute-start | bytes 786440 | tf_op jit(solution)/shard_map/ppermute | solution.py:446
  21.1 25.4 %collective-permute-start.16 = (f32[128,512]{1,0:T(8,128)S(1)}, f32[128,512]{1,0:T(8,128)S(1)}, u32[]{:S(2)}, u32[]{:S(2)}) collective-permute-start(f32[128,512]{1,0:T(8,128)S(1)} %pad_maximum_fusion.1), channel_id=1, source_target_pairs={{0,2},{1,3},{2,0},{3,1},{4,6},{5,7},{6,4},{7,5},{8,10},{9,11},{10,... | collective-permute-start | bytes 786440 | tf_op jit(solution)/shard_map/ppermute | solution.py:446
  23.7 22.7 %collective-permute-start.17 = (f32[128,512]{1,0:T(8,128)S(1)}, f32[128,512]{1,0:T(8,128)S(1)}, u32[]{:S(2)}, u32[]{:S(2)}) collective-permute-start(f32[128,512]{1,0:T(8,128)S(1)} %pad_maximum_fusion.1), channel_id=1, source_target_pairs={{0,3},{1,0},{2,1},{3,2},{4,7},{5,4},{6,5},{7,6},{8,11},{9,8},{10,9... | collective-permute-start | bytes 786440 | tf_op jit(solution)/shard_map/ppermute | solution.py:446
  30.6 7.7 %collective-permute-start = (f32[8,512]{1,0:T(8,128)S(1)}, f32[8,512]{1,0:T(8,128)S(1)}, u32[]{:S(2)}, u32[]{:S(2)}) collective-permute-start(f32[8,512]{1,0:T(8,128)S(1)} %reduce_sum.28), channel_id=1, source_target_pairs={{0,32},{32,0},{1,33},{33,1},{2,34},{34,2},{3,35},{35,3},{4,36},{36... | collective-permute-start | bytes 49160 | tf_op jit(solution)/shard_map/ppermute | solution.py:446
  38.3 5.7 %collective-permute-start.1 = (f32[16,512]{1,0:T(8,128)S(1)}, f32[16,512]{1,0:T(8,128)S(1)}, u32[]{:S(2)}, u32[]{:S(2)}) collective-permute-start(f32[16,512]{1,0:T(8,128)S(1)} %pad_maximum_fusion.2), channel_id=1, source_target_pairs={{0,64},{64,128},{128,192},{192,0},{1,65},{65,129},{129,193},{193,1... | collective-permute-start | bytes 98312 | tf_op jit(solution)/shard_map/ppermute | solution.py:446
  39.8 5.4 %collective-permute-start.2 = (f32[16,512]{1,0:T(8,128)S(1)}, f32[16,512]{1,0:T(8,128)S(1)}, u32[]{:S(2)}, u32[]{:S(2)}) collective-permute-start(f32[16,512]{1,0:T(8,128)S(1)} %pad_maximum_fusion.2), channel_id=1, source_target_pairs={{0,128},{64,192},{128,0},{192,64},{1,129},{65,193},{129,1},{193,65... | collective-permute-start | bytes 98312 | tf_op jit(solution)/shard_map/ppermute | solution.py:446
  42.5 3.9 %collective-permute-start.3 = (f32[16,512]{1,0:T(8,128)S(1)}, f32[16,512]{1,0:T(8,128)S(1)}, u32[]{:S(2)}, u32[]{:S(2)}) collective-permute-start(f32[16,512]{1,0:T(8,128)S(1)} %pad_maximum_fusion.2), channel_id=1, source_target_pairs={{0,192},{64,0},{128,64},{192,128},{1,193},{65,1},{129,65},{193,129... | collective-permute-start | bytes 98312 | tf_op jit(solution)/shard_map/ppermute | solution.py:446
  46.4 1.3 collective-permute-start.4
  46.5 28.8 %collective-permute-start.18 = (f32[512,512]{1,0:T(8,128)S(1)}, f32[512,512]{1,0:T(8,128)}, u32[]{:S(2)}, u32[]{:S(2)}) collective-permute-start(f32[512,512]{1,0:T(8,128)S(1)} %constant_dynamic-update-slice_fusion.18.na), channel_id=1, source_target_pairs={{0,16},{16,0},{1,17},{17,1},{2,18},{18,2},{3,19},{19,3},{4,20},{20... | collective-permute-start | bytes 3145736 | tf_op jit(solution)/shard_map/ppermute | solution.py:530
  48.8 29.0 %copy-start.4 = (f32[512,256]{1,0:T(8,128)S(1)}, f32[512,256]{1,0:T(8,128)}, u32[]{:S(2)}) copy-start(f32[512,256]{1,0:T(8,128)} %x_ref.1) | copy-start | bytes 1572868
  48.9 6.0 %collective-permute-start.5 = (f32[32,512]{1,0:T(8,128)S(1)}, f32[32,512]{1,0:T(8,128)S(1)}, u32[]{:S(2)}, u32[]{:S(2)}) collective-permute-start(f32[32,512]{1,0:T(8,128)S(1)} %get-tuple-element.38), channel_id=1, source_target_pairs={{0,4},{4,8},{8,12},{12,0},{1,5},{5,9},{9,13},{13,1},{2,6},{6,10},{... | collective-permute-start | bytes 196616 | tf_op jit(solution)/shard_map/ppermute | solution.py:446
  50.4 5.5 %collective-permute-start.6 = (f32[32,512]{1,0:T(8,128)S(1)}, f32[32,512]{1,0:T(8,128)S(1)}, u32[]{:S(2)}, u32[]{:S(2)}) collective-permute-start(f32[32,512]{1,0:T(8,128)S(1)} %get-tuple-element.38), channel_id=1, source_target_pairs={{0,8},{4,12},{8,0},{12,4},{1,9},{5,13},{9,1},{13,5},{2,10},{6,14},... | collective-permute-start | bytes 196616 | tf_op jit(solution)/shard_map/ppermute | solution.py:446
  51.4 6.4 %collective-permute-start.7 = (f32[32,512]{1,0:T(8,128)S(1)}, f32[32,512]{1,0:T(8,128)S(1)}, u32[]{:S(2)}, u32[]{:S(2)}) collective-permute-start(f32[32,512]{1,0:T(8,128)S(1)} %get-tuple-element.38), channel_id=1, source_target_pairs={{0,12},{4,0},{8,4},{12,8},{1,13},{5,1},{9,5},{13,9},{2,14},{6,2},{... | collective-permute-start | bytes 196616 | tf_op jit(solution)/shard_map/ppermute | solution.py:446
  57.8 9.4 %collective-permute-start.8 = (f32[128,512]{1,0:T(8,128)S(1)}, f32[128,512]{1,0:T(8,128)S(1)}, u32[]{:S(2)}, u32[]{:S(2)}) collective-permute-start(f32[128,512]{1,0:T(8,128)S(1)} %pad_maximum_fusion), channel_id=1, source_target_pairs={{0,1},{1,2},{2,3},{3,0},{4,5},{5,6},{6,7},{7,4},{8,9},{9,10},{10,1... | collective-permute-start | bytes 786440 | tf_op jit(solution)/shard_map/ppermute | solution.py:446
  58.5 16.5 %collective-permute-start.9 = (f32[128,512]{1,0:T(8,128)S(1)}, f32[128,512]{1,0:T(8,128)S(1)}, u32[]{:S(2)}, u32[]{:S(2)}) collective-permute-start(f32[128,512]{1,0:T(8,128)S(1)} %pad_maximum_fusion), channel_id=1, source_target_pairs={{0,2},{1,3},{2,0},{3,1},{4,6},{5,7},{6,4},{7,5},{8,10},{9,11},{10,... | collective-permute-start | bytes 786440 | tf_op jit(solution)/shard_map/ppermute | solution.py:446
  63.6 11.5 %collective-permute-start.10 = (f32[128,512]{1,0:T(8,128)S(1)}, f32[128,512]{1,0:T(8,128)S(1)}, u32[]{:S(2)}, u32[]{:S(2)}) collective-permute-start(f32[128,512]{1,0:T(8,128)S(1)} %pad_maximum_fusion), channel_id=1, source_target_pairs={{0,3},{1,0},{2,1},{3,2},{4,7},{5,4},{6,5},{7,6},{8,11},{9,8},{10,9... | collective-permute-start | bytes 786440 | tf_op jit(solution)/shard_map/ppermute | solution.py:446
  75.1 2.7 collective-permute-start.11

commit v4 on v3

--- a/solution.py
+++ b/solution.py
@@ -442,10 +442,9 @@
 
 
 def ring_gather(value, axis, size):
-    parts = [value] + [
-        lax.ppermute(value, axis, [(i, (i + k) % size) for i in range(size)])
-        for k in range(1, size)
-    ]
+    parts = [value]
+    for k in range(1, size):
+        parts.append(lax.ppermute(value, axis, [(i, (i + k) % size) for i in range(size)]))
     return jnp.concatenate(parts, axis=0)
 
 

time: 382 us -> 382 us (level)
  no operation moved by 1% of the time
where the time goes in v4:
time: 382 us; the launch traced here: 381 us
  Pallas kernels  308 us (81%)
  starting transfers between devices  41.2 us (11%)
  waiting for transfers between devices  26.9 us (7%)
    pallas_call x4, Pallas kernels, call(): pl.pallas_call(kernel, out_shape=shapes, in_specs=[smem] + [vmem] * (len(...  308 us
    ppermute x17, starting transfers between devices, ring_gather(): lax.ppermute(value, axis, [(i, (i + k) % size) for i in range(size)])  34.6 us
    ppermute x17, waiting for transfers between devices, ring_gather(): lax.ppermute(value, axis, [(i, (i + k) % size) for i in range(size)])  24.3 us
  transfers between devices with their start and end apart: 20, of which 11 were waited for; matrix products, arithmetic and copies ran while one was open for 0% of the time, Pallas kernels for 1%

profile of v4, /device:TPU:32, one launch (start us, length us, event | category | flops | bytes accessed | tf_op | source)
XLA Modules:
  0.0 381.3 jit_solution(16851249101327610483)
XLA Ops:
  0.0 0.9 copy-done
  2.3 1.7 shard_map.55
  4.0 2.0 collective-permute-start.12
  6.0 2.3 collective-permute-start.13
  8.3 1.1 collective-permute-start.14
  9.5 2.4 shard_map.56
  11.9 5.9 %all-to-all-start.2 = ((f32[16,8,512]{2,1,0:T(8,128)}), f32[16,8,512]{2,1,0:T(8,128)S(1)}, u32[]{:S(2)}, u32[]{:S(2)}) async-start(f32[16,8,512]{2,1,0:T(8,128)} %bitcast.12), calls=%async_computation.2 | async-start | bytes 524288 | tf_op jit(solution)/shard_map/all_to_all | solution.py:489
  19.5 1.5 collective-permute-start.15
  21.1 2.7 collective-permute-start.16
  23.7 1.5 collective-permute-start.17
  25.2 5.2 %collective-permute-done.15 = f32[128,512]{1,0:T(8,128)S(1)} collective-permute-done((f32[128,512]{1,0:T(8,128)S(1)}, f32[128,512]{1,0:T(8,128)S(1)}, u32[]{:S(2)}, u32[]{:S(2)}) %collective-permute-start.15) | collective-permute-done | bytes 262176 | tf_op jit(solution)/shard_map/ppermute | solution.py:447
  30.6 5.9 %collective-permute-start = (f32[8,512]{1,0:T(8,128)S(1)}, f32[8,512]{1,0:T(8,128)S(1)}, u32[]{:S(2)}, u32[]{:S(2)}) collective-permute-start(f32[8,512]{1,0:T(8,128)S(1)} %reduce_sum.28), channel_id=1, source_target_pairs={{0,32},{32,0},{1,33},{33,1},{2,34},{34,2},{3,35},{35,3},{4,36},{36... | collective-permute-start | bytes 49160 | tf_op jit(solution)/shard_map/ppermute | solution.py:447
  36.5 1.8 collective-permute-done
  38.3 1.5 collective-permute-start.1
  39.8 2.7 collective-permute-start.2
  42.5 1.4 collective-permute-start.3
  44.0 1.2 collective-permute-done.2
  45.2 1.2 collective-permute-done.3
  47.8 0.9 shard_map.57
  48.9 1.5 collective-permute-start.5
  50.4 1.0 collective-permute-start.6
  51.4 1.2 collective-permute-start.7
  52.6 2.3 collective-permute-done.5
  54.9 1.0 collective-permute-done.6
  55.9 1.9 collective-permute-done.7
  57.8 0.7 collective-permute-start.8
  58.5 5.0 %collective-permute-start.9 = (f32[128,512]{1,0:T(8,128)S(1)}, f32[128,512]{1,0:T(8,128)S(1)}, u32[]{:S(2)}, u32[]{:S(2)}) collective-permute-start(f32[128,512]{1,0:T(8,128)S(1)} %pad_maximum_fusion), channel_id=1, source_target_pairs={{0,2},{1,3},{2,0},{3,1},{4,6},{5,7},{6,4},{7,5},{8,10},{9,11},{10,... | collective-permute-start | bytes 786440 | tf_op jit(solution)/shard_map/ppermute | solution.py:447
  63.6 2.5 collective-permute-start.10
  66.1 1.1 collective-permute-done.8
  67.2 7.8 %collective-permute-done.9 = f32[128,512]{1,0:T(8,128)S(1)} collective-permute-done((f32[128,512]{1,0:T(8,128)S(1)}, f32[128,512]{1,0:T(8,128)S(1)}, u32[]{:S(2)}, u32[]{:S(2)}) %collective-permute-start.9) | collective-permute-done | bytes 262176 | tf_op jit(solution)/shard_map/ppermute | solution.py:447
  75.3 2.6 collective-permute-done.11.ob
  77.9 303.4 %shard_map.58 = f32[512,256]{1,0:T(8,128)} custom-call(s32[4]{0:T(128)S(1)} %pad_add_fusion.1.where_ref, f32[8,512]{1,0:T(8,128)S(1)} %get-tuple-element.26.par_ref, f32[512,512]{1,0:T(8,128)S(1)} %constant_dynamic-update-slice_fusion.11.oa, f32[512,512]{1,0:T(8,128)S(1)} %collective-permute-done.11.ob, ...), custom_call_target="tpu_custom_call" | custom-call | flops 21474836480 | bytes 4194304 | tf_op jit(solution)/shard_map/pallas_call | solution.py:475
  (56 shorter events, 4.2 us)
Async XLA Ops:
  0.0 9.5 %copy-start.5 = (s32[2,512]{1,0:T(2,128)S(1)}, s32[2,512]{1,0:T(2,128)}, u32[]{:S(2)}) copy-start(s32[2,512]{1,0:T(2,128)} %index_ref.5) | copy-start | bytes 12292
  0.0 0.9 copy-start
  0.9 0.7 copy-start.1
  1.6 0.7 copy-start.2
  2.3 7.2 %copy-start.3 = (f32[512,256]{1,0:T(8,128)S(1)}, f32[512,256]{1,0:T(8,128)}, u32[]{:S(2)}) copy-start(f32[512,256]{1,0:T(8,128)} %x_ref.1) | copy-start | bytes 1572868
  4.0 15.5 %collective-permute-start.12 = (f32[32,512]{1,0:T(8,128)S(1)}, f32[32,512]{1,0:T(8,128)S(1)}, u32[]{:S(2)}, u32[]{:S(2)}) collective-permute-start(f32[32,512]{1,0:T(8,128)S(1)} %bitcast.15), channel_id=1, source_target_pairs={{0,4},{4,8},{8,12},{12,0},{1,5},{5,9},{9,13},{13,1},{2,6},{6,10},{... | collective-permute-start | bytes 196616 | tf_op jit(solution)/shard_map/ppermute | solution.py:447
  6.0 13.5 %collective-permute-start.13 = (f32[32,512]{1,0:T(8,128)S(1)}, f32[32,512]{1,0:T(8,128)S(1)}, u32[]{:S(2)}, u32[]{:S(2)}) collective-permute-start(f32[32,512]{1,0:T(8,128)S(1)} %bitcast.16), channel_id=1, source_target_pairs={{0,8},{4,12},{8,0},{12,4},{1,9},{5,13},{9,1},{13,5},{2,10},{6,14},... | collective-permute-start | bytes 196616 | tf_op jit(solution)/shard_map/ppermute | solution.py:447
  8.3 11.2 %collective-permute-start.14 = (f32[32,512]{1,0:T(8,128)S(1)}, f32[32,512]{1,0:T(8,128)S(1)}, u32[]{:S(2)}, u32[]{:S(2)}) collective-permute-start(f32[32,512]{1,0:T(8,128)S(1)} %bitcast.17), channel_id=1, source_target_pairs={{0,12},{4,0},{8,4},{12,8},{1,13},{5,1},{9,5},{13,9},{2,14},{6,2},{... | collective-permute-start | bytes 196616 | tf_op jit(solution)/shard_map/ppermute | solution.py:447
  11.9 18.6 %all-to-all-start.2 = ((f32[16,8,512]{2,1,0:T(8,128)}), f32[16,8,512]{2,1,0:T(8,128)S(1)}, u32[]{:S(2)}, u32[]{:S(2)}) async-start(f32[16,8,512]{2,1,0:T(8,128)} %bitcast.12), calls=%async_computation.2 | async-start | bytes 524288 | tf_op jit(solution)/shard_map/all_to_all | solution.py:489
  19.5 11.0 %collective-permute-start.15 = (f32[128,512]{1,0:T(8,128)S(1)}, f32[128,512]{1,0:T(8,128)S(1)}, u32[]{:S(2)}, u32[]{:S(2)}) collective-permute-start(f32[128,512]{1,0:T(8,128)S(1)} %pad_maximum_fusion.1), channel_id=1, source_target_pairs={{0,1},{1,2},{2,3},{3,0},{4,5},{5,6},{6,7},{7,4},{8,9},{9,10},{10,1... | collective-permute-start | bytes 786440 | tf_op jit(solution)/shard_map/ppermute | solution.py:447
  21.1 25.4 %collective-permute-start.16 = (f32[128,512]{1,0:T(8,128)S(1)}, f32[128,512]{1,0:T(8,128)S(1)}, u32[]{:S(2)}, u32[]{:S(2)}) collective-permute-start(f32[128,512]{1,0:T(8,128)S(1)} %pad_maximum_fusion.1), channel_id=1, source_target_pairs={{0,2},{1,3},{2,0},{3,1},{4,6},{5,7},{6,4},{7,5},{8,10},{9,11},{10,... | collective-permute-start | bytes 786440 | tf_op jit(solution)/shard_map/ppermute | solution.py:447
  23.7 22.7 %collective-permute-start.17 = (f32[128,512]{1,0:T(8,128)S(1)}, f32[128,512]{1,0:T(8,128)S(1)}, u32[]{:S(2)}, u32[]{:S(2)}) collective-permute-start(f32[128,512]{1,0:T(8,128)S(1)} %pad_maximum_fusion.1), channel_id=1, source_target_pairs={{0,3},{1,0},{2,1},{3,2},{4,7},{5,4},{6,5},{7,6},{8,11},{9,8},{10,9... | collective-permute-start | bytes 786440 | tf_op jit(solution)/shard_map/ppermute | solution.py:447
  30.6 7.7 %collective-permute-start = (f32[8,512]{1,0:T(8,128)S(1)}, f32[8,512]{1,0:T(8,128)S(1)}, u32[]{:S(2)}, u32[]{:S(2)}) collective-permute-start(f32[8,512]{1,0:T(8,128)S(1)} %reduce_sum.28), channel_id=1, source_target_pairs={{0,32},{32,0},{1,33},{33,1},{2,34},{34,2},{3,35},{35,3},{4,36},{36... | collective-permute-start | bytes 49160 | tf_op jit(solution)/shard_map/ppermute | solution.py:447
  38.3 5.7 %collective-permute-start.1 = (f32[16,512]{1,0:T(8,128)S(1)}, f32[16,512]{1,0:T(8,128)S(1)}, u32[]{:S(2)}, u32[]{:S(2)}) collective-permute-start(f32[16,512]{1,0:T(8,128)S(1)} %pad_maximum_fusion.2), channel_id=1, source_target_pairs={{0,64},{64,128},{128,192},{192,0},{1,65},{65,129},{129,193},{193,1... | collective-permute-start | bytes 98312 | tf_op jit(solution)/shard_map/ppermute | solution.py:447
  39.8 5.4 %collective-permute-start.2 = (f32[16,512]{1,0:T(8,128)S(1)}, f32[16,512]{1,0:T(8,128)S(1)}, u32[]{:S(2)}, u32[]{:S(2)}) collective-permute-start(f32[16,512]{1,0:T(8,128)S(1)} %pad_maximum_fusion.2), channel_id=1, source_target_pairs={{0,128},{64,192},{128,0},{192,64},{1,129},{65,193},{129,1},{193,65... | collective-permute-start | bytes 98312 | tf_op jit(solution)/shard_map/ppermute | solution.py:447
  42.5 3.9 %collective-permute-start.3 = (f32[16,512]{1,0:T(8,128)S(1)}, f32[16,512]{1,0:T(8,128)S(1)}, u32[]{:S(2)}, u32[]{:S(2)}) collective-permute-start(f32[16,512]{1,0:T(8,128)S(1)} %pad_maximum_fusion.2), channel_id=1, source_target_pairs={{0,192},{64,0},{128,64},{192,128},{1,193},{65,1},{129,65},{193,129... | collective-permute-start | bytes 98312 | tf_op jit(solution)/shard_map/ppermute | solution.py:447
  46.4 1.3 collective-permute-start.4
  46.5 28.8 %collective-permute-start.18 = (f32[512,512]{1,0:T(8,128)S(1)}, f32[512,512]{1,0:T(8,128)}, u32[]{:S(2)}, u32[]{:S(2)}) collective-permute-start(f32[512,512]{1,0:T(8,128)S(1)} %constant_dynamic-update-slice_fusion.18.na), channel_id=1, source_target_pairs={{0,16},{16,0},{1,17},{17,1},{2,18},{18,2},{3,19},{19,3},{4,20},{20... | collective-permute-start | bytes 3145736 | tf_op jit(solution)/shard_map/ppermute | solution.py:529
  48.8 29.0 %copy-start.4 = (f32[512,256]{1,0:T(8,128)S(1)}, f32[512,256]{1,0:T(8,128)}, u32[]{:S(2)}) copy-start(f32[512,256]{1,0:T(8,128)} %x_ref.1) | copy-start | bytes 1572868
  48.9 6.0 %collective-permute-start.5 = (f32[32,512]{1,0:T(8,128)S(1)}, f32[32,512]{1,0:T(8,128)S(1)}, u32[]{:S(2)}, u32[]{:S(2)}) collective-permute-start(f32[32,512]{1,0:T(8,128)S(1)} %get-tuple-element.38), channel_id=1, source_target_pairs={{0,4},{4,8},{8,12},{12,0},{1,5},{5,9},{9,13},{13,1},{2,6},{6,10},{... | collective-permute-start | bytes 196616 | tf_op jit(solution)/shard_map/ppermute | solution.py:447
  50.4 5.5 %collective-permute-start.6 = (f32[32,512]{1,0:T(8,128)S(1)}, f32[32,512]{1,0:T(8,128)S(1)}, u32[]{:S(2)}, u32[]{:S(2)}) collective-permute-start(f32[32,512]{1,0:T(8,128)S(1)} %get-tuple-element.38), channel_id=1, source_target_pairs={{0,8},{4,12},{8,0},{12,4},{1,9},{5,13},{9,1},{13,5},{2,10},{6,14},... | collective-permute-start | bytes 196616 | tf_op jit(solution)/shard_map/ppermute | solution.py:447
  51.4 6.4 %collective-permute-start.7 = (f32[32,512]{1,0:T(8,128)S(1)}, f32[32,512]{1,0:T(8,128)S(1)}, u32[]{:S(2)}, u32[]{:S(2)}) collective-permute-start(f32[32,512]{1,0:T(8,128)S(1)} %get-tuple-element.38), channel_id=1, source_target_pairs={{0,12},{4,0},{8,4},{12,8},{1,13},{5,1},{9,5},{13,9},{2,14},{6,2},{... | collective-permute-start | bytes 196616 | tf_op jit(solution)/shard_map/ppermute | solution.py:447
  57.8 9.4 %collective-permute-start.8 = (f32[128,512]{1,0:T(8,128)S(1)}, f32[128,512]{1,0:T(8,128)S(1)}, u32[]{:S(2)}, u32[]{:S(2)}) collective-permute-start(f32[128,512]{1,0:T(8,128)S(1)} %pad_maximum_fusion), channel_id=1, source_target_pairs={{0,1},{1,2},{2,3},{3,0},{4,5},{5,6},{6,7},{7,4},{8,9},{9,10},{10,1... | collective-permute-start | bytes 786440 | tf_op jit(solution)/shard_map/ppermute | solution.py:447
  58.5 16.5 %collective-permute-start.9 = (f32[128,512]{1,0:T(8,128)S(1)}, f32[128,512]{1,0:T(8,128)S(1)}, u32[]{:S(2)}, u32[]{:S(2)}) collective-permute-start(f32[128,512]{1,0:T(8,128)S(1)} %pad_maximum_fusion), channel_id=1, source_target_pairs={{0,2},{1,3},{2,0},{3,1},{4,6},{5,7},{6,4},{7,5},{8,10},{9,11},{10,... | collective-permute-start | bytes 786440 | tf_op jit(solution)/shard_map/ppermute | solution.py:447
  63.6 11.5 %collective-permute-start.10 = (f32[128,512]{1,0:T(8,128)S(1)}, f32[128,512]{1,0:T(8,128)S(1)}, u32[]{:S(2)}, u32[]{:S(2)}) collective-permute-start(f32[128,512]{1,0:T(8,128)S(1)} %pad_maximum_fusion), channel_id=1, source_target_pairs={{0,3},{1,0},{2,1},{3,2},{4,7},{5,4},{6,5},{7,6},{8,11},{9,8},{10,9... | collective-permute-start | bytes 786440 | tf_op jit(solution)/shard_map/ppermute | solution.py:447
  75.1 2.7 collective-permute-start.11
